TPU v7x, 32 devices: a whole 2x2x4 slice. The times are simulated.
32 devices in a mesh: replica: 1, ctx: 32 (over z, y, x, core).
Axes of the slice: x: 2, y: 2, z: 4, core: 2. Of those that a mesh axis runs over, the one named last changes fastest.
Arguments:
- queries: bfloat16 [128, 4096], P(('replica', 'ctx')), may hold values from -4 to 6.2
- own_key: bfloat16 [128, 256], P(('replica', 'ctx')), may hold values from -12 to 12
- own_value: bfloat16 [128, 256], P(('replica', 'ctx')), may hold values from -40 to 40
- cache_keys: bfloat16 [2, 1024, 256], P('replica', 'ctx'), may hold values from -4 to 4.7
- cache_values: bfloat16 [2, 1024, 256], P('replica', 'ctx'), may hold values from -40 to 40
- prefix_of_row: int32 [128], P('replica'), may hold values from 0 to 1, as said below
- context_len: int32 [2], P('replica'), may hold values from 512 to 1024
- hidden_in: bfloat16 [128, 4096], P(('replica', 'ctx')), may hold values from -3 to 3
- w_out: bfloat16 [4096, 4096], P('ctx'), may hold values from -0.09375 to 0.09375
- norm_gain: float32 [4096], replicated, may hold values from 0.5 to 1.5
- expert_ids: int32 [128, 8], P(('replica', 'ctx')), may hold values from 0 to 15, all different within a row; in each aligned block of 4 rows (0 to 3, 4 to 7, ...) at most 4 rows name the same one
- route_weights: float32 [128, 8], P(('replica', 'ctx')), may hold values from 0.05 to 0.4
- gate_up_codes: bfloat16 [32, 4096, 768], P('ctx'), may hold values from -0.09375 to 0.09375
- gate_up_scales: float32 [32, 32, 6], P('ctx'), may hold values from 0.6 to 1.7
- down_codes: bfloat16 [32, 384, 4096], P('ctx'), may hold values from -0.21875 to 0.21875
- down_scales: float32 [32, 3, 32], P('ctx'), may hold values from 0.6 to 1.7
Outputs:
- attention_out: bfloat16 [128, 4096], P(('replica', 'ctx'))
- layer_out: bfloat16 [128, 4096], P(('replica', 'ctx'))
Inputs may be any that keep to these rules, and one draw needn't show every extreme that they name: `prefix_of_row`: the rows come in aligned blocks of 64 consecutive rows that all name one prefix. `expert_ids`: each row names 8 different experts; among the 4 rows of one device no expert is named more than 4 times.
All inputs are finite; a program needn't handle non-finite values.
Results may differ from a plain program's by a relative error of at most 0.014.
Values may be sent and summed in bfloat16 or wider, within the bound.
A program may use at most 128 MiB of HBM per device.

v0:
```python
import math

import jax
import jax.numpy as jnp
from jax import lax
from jax.experimental import pallas as pl
from jax.experimental.pallas import tpu as pltpu
from jax.sharding import PartitionSpec as P

HD = 128
CAND = 64


NEG = -1e30
EPSILON = 1e-06


def swapped(value, axis, distance):
    return lax.ppermute(value, axis, [(i, i ^ 1 << distance) for i in range(lax.axis_size(axis))])


def dequantize(code_values, scales):
    rows_per = code_values.shape[0] // scales.shape[0]
    cols_per = code_values.shape[1] // scales.shape[1]
    spread = jnp.repeat(jnp.repeat(scales, rows_per, axis=0), cols_per, axis=1)
    return (code_values.astype(jnp.float32) * spread).astype(jnp.bfloat16)


def block_partials(query_heads, key_heads, value_heads, is_valid, score_scale):
    scores = (
        jnp.einsum(
            "brgqd,bstgd->brgqst", query_heads, key_heads, preferred_element_type=jnp.float32
        )
        * score_scale
    )
    valid_full = is_valid[:, None, None, None, :, :]
    masked = jnp.where(valid_full, scores, NEG)
    block_max = jnp.max(masked, axis=-1)
    weights = jnp.where(valid_full, jnp.exp(masked - block_max[..., None]), 0.0)
    block_total = jnp.sum(weights, axis=-1)
    numerator = jnp.einsum(
        "brgqst,bstgd->brgqsd",
        weights.astype(jnp.bfloat16),
        value_heads,
        preferred_element_type=jnp.float32,
    )
    block_out = (numerator / jnp.maximum(block_total, 1.0)[..., None]).astype(jnp.bfloat16)
    return (block_max, block_total, block_out)


def fold_blocks(block_max, block_total, block_out):
    local_top = jnp.max(block_max, axis=-1)
    factor = block_total * jnp.exp(block_max - local_top[..., None])
    numer = jnp.sum(factor[..., None] * block_out.astype(jnp.float32), axis=-2)
    denom = jnp.sum(factor, axis=-1)
    return (local_top, numer, denom)


def merge_pair(first, second):
    top = jnp.maximum(first[0], second[0])
    scale_first = jnp.exp(first[0] - top)
    scale_second = jnp.exp(second[0] - top)
    numer = first[1] * scale_first[..., None] + second[1] * scale_second[..., None]
    denom = first[2] * scale_first + second[2] * scale_second
    return (top, numer, denom)


def flipped(index, pattern, bits):
    total = 0
    for bit in range(bits):
        value = index // (1 << bit) % 2
        if pattern >> bit & 1:
            value = 1 - value
        total = total + value * (1 << bit)
    return total


def greet(me, bits):
    barrier = pltpu.get_barrier_semaphore()
    for bit in range(bits):
        pl.semaphore_signal(
            barrier,
            inc=1,
            device_id={"ctx": flipped(me, 1 << bit, bits)},
            device_id_type=pl.DeviceIdType.MESH,
        )
    pl.semaphore_wait(barrier, bits)


def lane_parts(rows, bits):
    middle = rows // 32 * 16
    first = list(range(bits))
    second = list(range(bits))
    if bits > 2:
        second[1], second[2] = second[2], second[1]
    return ((0, middle, first), (middle, rows - middle, second))


def gather_kernel(bits, block_ref, out_ref, send_sem, recv_sem, own_sem):
    me = lax.axis_index("ctx")
    parts = lane_parts(block_ref.shape[0], bits)
    own = pltpu.make_async_copy(block_ref, out_ref.at[me], own_sem)
    own.start()
    greet(me, bits)
    copies = [{}, {}]
    waited = [set(), set()]
    for step in range(bits):
        for part, (start, size, order) in enumerate(parts):
            bit = order[bits - 1 - step]
            held = [0]
            for earlier in range(step):
                held = held + [p | 1 << order[bits - 1 - earlier] for p in held]
            for pattern in held:
                block = flipped(me, pattern, bits)
                if pattern:
                    if pattern not in waited[part]:
                        copies[part][pattern].wait_recv()
                        waited[part].add(pattern)
                    source = out_ref.at[block, pl.ds(start, size)]
                else:
                    source = block_ref.at[pl.ds(start, size)]
                slot = pattern | 1 << bit
                copy = pltpu.make_async_remote_copy(
                    src_ref=source,
                    dst_ref=out_ref.at[block, pl.ds(start, size)],
                    send_sem=send_sem.at[part, slot],
                    recv_sem=recv_sem.at[part, slot],
                    device_id={"ctx": flipped(me, 1 << bit, bits)},
                    device_id_type=pl.DeviceIdType.MESH,
                )
                copy.start()
                copies[part][slot] = copy
    for part in range(2):
        for slot, copy in copies[part].items():
            if slot not in waited[part]:
                copy.wait_recv()
            copy.wait_send()
    own.wait()


def gather_blocks(block, collective_id):
    shards = lax.axis_size("ctx")
    bits = shards.bit_length() - 1
    return pl.pallas_call(
        lambda *refs: gather_kernel(bits, *refs),
        out_shape=jax.ShapeDtypeStruct((shards,) + block.shape, block.dtype),
        in_specs=[pl.BlockSpec(memory_space=pltpu.VMEM)],
        out_specs=pl.BlockSpec(memory_space=pltpu.VMEM),
        scratch_shapes=[
            pltpu.SemaphoreType.DMA((2, shards)),
            pltpu.SemaphoreType.DMA((2, shards)),
            pltpu.SemaphoreType.DMA,
        ],
        compiler_params=pltpu.CompilerParams(collective_id=collective_id, has_side_effects=True),
        name="gather_blocks",
    )(block)


def scatter_kernel(bits, blocks_ref, out_ref, outbox, inbox, send_sem, recv_sem):
    me = lax.axis_index("ctx")
    shards = 1 << bits
    parts = lane_parts(blocks_ref.shape[1], bits)
    greet(me, bits)
    arrived = [{p: [] for p in range(shards)} for _ in parts]
    pending = [{}, {}]
    finished = [set(), set()]
    sent = []
    next_slot = [0, 0]

    def total(part, pattern):
        start, size, _ = parts[part]
        value = blocks_ref[flipped(me, pattern, bits), pl.ds(start, size), :].astype(jnp.float32)
        for slot in arrived[part][pattern]:
            if slot not in finished[part]:
                pending[part][slot].wait_recv()
                finished[part].add(slot)
            value = value + inbox[slot, pl.ds(start, size), :].astype(jnp.float32)
        return value

    for step in range(bits):
        fresh = []
        for part, (start, size, order) in enumerate(parts):
            bit = order[step]
            done_mask = sum(1 << b for b in order[:step])
            for pattern in range(shards):
                if pattern & done_mask or not pattern >> bit & 1:
                    continue
                slot = next_slot[part]
                next_slot[part] += 1
                if step:
                    outbox[slot, pl.ds(start, size), :] = total(part, pattern).astype(outbox.dtype)
                    source = outbox.at[slot, pl.ds(start, size)]
                else:
                    source = blocks_ref.at[flipped(me, pattern, bits), pl.ds(start, size)]
                copy = pltpu.make_async_remote_copy(
                    src_ref=source,
                    dst_ref=inbox.at[slot, pl.ds(start, size)],
                    send_sem=send_sem.at[part, slot],
                    recv_sem=recv_sem.at[part, slot],
                    device_id={"ctx": flipped(me, 1 << bit, bits)},
                    device_id_type=pl.DeviceIdType.MESH,
                )
                copy.start()
                pending[part][slot] = copy
                sent.append(copy)
                fresh.append((part, pattern ^ 1 << bit, slot))
        for part, pattern, slot in fresh:
            arrived[part][pattern].append(slot)
    for part, (start, size, _) in enumerate(parts):
        out_ref[pl.ds(start, size), :] = total(part, 0)
    for copy in sent:
        copy.wait_send()


def scatter_sum(blocks, collective_id):
    shards = lax.axis_size("ctx")
    bits = shards.bit_length() - 1
    return pl.pallas_call(
        lambda *refs: scatter_kernel(bits, *refs),
        out_shape=jax.ShapeDtypeStruct(blocks.shape[1:], jnp.float32),
        in_specs=[pl.BlockSpec(memory_space=pltpu.VMEM)],
        out_specs=pl.BlockSpec(memory_space=pltpu.VMEM),
        scratch_shapes=[
            pltpu.VMEM(blocks.shape, blocks.dtype),
            pltpu.VMEM(blocks.shape, blocks.dtype),
            pltpu.SemaphoreType.DMA((2, shards)),
            pltpu.SemaphoreType.DMA((2, shards)),
        ],
        compiler_params=pltpu.CompilerParams(collective_id=collective_id, has_side_effects=True),
        name="scatter_sum",
    )(blocks)


def local(
    queries,
    own_key,
    own_value,
    cache_keys,
    cache_values,
    prefix_of_row,
    context_len,
    hidden_in,
    w_out,
    norm_gain,
    expert_ids,
    route_weights,
    gate_up_codes,
    gate_up_scales,
    down_codes,
    down_scales,
):
    shards = lax.axis_size("ctx")
    device = lax.axis_index("ctx")
    head_size = HD
    local_rows = queries.shape[0]
    key_groups = own_key.shape[1] // head_size
    per_group = queries.shape[1] // own_key.shape[1]
    head_count = key_groups * per_group
    ctx_local = cache_keys.shape[1]
    key_width = cache_keys.shape[2]
    score_scale = 1.0 / math.sqrt(head_size)
    block_prefix = prefix_of_row.reshape(-1, CAND)[:, 0]
    prefix_count = block_prefix.shape[0]
    group_size = CAND // local_rows
    group_bits = group_size.bit_length() - 1
    prefix_bits = (shards // group_size).bit_length() - 1
    group_index = device // group_size
    member = device % group_size
    relay = jnp.concatenate(
        [jnp.take(cache_keys, block_prefix, axis=0), jnp.take(cache_values, block_prefix, axis=0)],
        axis=-1,
    )
    relay_shape = relay.shape
    for bit in range(prefix_bits):
        low = 1 << bit
        view = relay.reshape((relay_shape[0] // (2 * low), 2, low) + relay_shape[1:])
        own_bit = group_index // low % 2
        sent = lax.dynamic_index_in_dim(view, 1 - own_bit, 1, False)
        got = swapped(sent, "ctx", group_bits + bit)
        view = lax.dynamic_update_index_in_dim(view, got, 1 - own_bit, 1)
        relay = view.reshape(relay_shape)
    held = queries
    for bit in range(group_bits):
        other = swapped(held, "ctx", bit)
        upper = device // (1 << bit) % 2
        held = jnp.where(
            upper == 0, jnp.concatenate([held, other], 0), jnp.concatenate([other, held], 0)
        )
    length = jnp.take(context_len, jnp.take(block_prefix, group_index))
    source_block = jnp.arange(prefix_count, dtype=jnp.int32) * group_size + member
    position = source_block[:, None] * ctx_local + jnp.arange(ctx_local, dtype=jnp.int32)[None, :]
    is_valid = (position < length)[None]
    query_heads = held.reshape(1, CAND, key_groups, per_group, head_size)
    key_heads = relay[..., :key_width].reshape(1, prefix_count, ctx_local, key_groups, head_size)
    value_heads = relay[..., key_width:].reshape(1, prefix_count, ctx_local, key_groups, head_size)
    block_max, block_total, block_out = block_partials(
        query_heads, key_heads, value_heads, is_valid, score_scale
    )
    block_max = block_max.reshape(CAND, head_count, prefix_count)
    block_total = block_total.reshape(CAND, head_count, prefix_count)
    block_out = block_out.reshape(CAND, head_count, prefix_count, head_size)
    state = fold_blocks(block_max, block_total, block_out)
    for bit in reversed(range(group_bits)):
        own_bit = device // (1 << bit) % 2
        parts = tuple((item.reshape((2, item.shape[0] // 2) + item.shape[1:]) for item in state))
        sent = tuple((lax.dynamic_index_in_dim(item, 1 - own_bit, 0, False) for item in parts))
        kept = tuple((lax.dynamic_index_in_dim(item, own_bit, 0, False) for item in parts))
        got = swapped(sent, "ctx", bit)
        state = merge_pair(kept, got)
    merged_top, merged_numer, merged_denom = state
    own_heads = queries.reshape(local_rows, key_groups, per_group, head_size)
    own_keys = own_key.reshape(local_rows, key_groups, head_size)
    own_score = (
        jnp.einsum(
            "rgqd,rgd->rgq", own_heads, own_keys, preferred_element_type=jnp.float32
        ).reshape(local_rows, head_count)
        * score_scale
    )
    top_score = jnp.maximum(merged_top, own_score)
    block_scale = jnp.exp(merged_top - top_score)
    own_weight = jnp.exp(own_score - top_score)
    own_term = own_value.reshape(local_rows, key_groups, 1, head_size).astype(
        jnp.float32
    ) * own_weight.reshape(local_rows, key_groups, per_group, 1)
    numerator_all = merged_numer * block_scale[..., None] + own_term.reshape(
        local_rows, head_count, head_size
    )
    denominator = merged_denom * block_scale + own_weight
    attended = (numerator_all / denominator[..., None]).reshape(local_rows, -1).astype(jnp.bfloat16)
    feature_width = hidden_in.shape[1]
    lanes = feature_width // 128
    head_rows = lax.all_to_all(attended, "ctx", split_axis=1, concat_axis=0, tiled=True)
    partial = jnp.dot(head_rows, w_out, preferred_element_type=jnp.float32).astype(jnp.bfloat16)
    projected = scatter_sum(partial.reshape(shards, local_rows * lanes, 128), 1).reshape(
        local_rows, feature_width
    )
    mixed_rows = hidden_in.astype(jnp.float32) + projected
    attention_out = mixed_rows.astype(jnp.bfloat16)
    mean_square = jnp.mean(mixed_rows * mixed_rows, axis=-1, keepdims=True)
    normed = (mixed_rows * lax.rsqrt(mean_square + EPSILON) * norm_gain).astype(jnp.bfloat16)
    experts_all = shards // 2
    chosen = expert_ids[:, :, None] == jnp.arange(experts_all, dtype=jnp.int32)[None, None, :]
    dense = jnp.sum(jnp.where(chosen, route_weights[:, :, None], 0.0), axis=1)
    coarse = lax.reduce_precision(dense, exponent_bits=8, mantissa_bits=7)
    fine = dense - coarse
    weight_cols = jnp.concatenate([coarse, fine], axis=1).astype(jnp.bfloat16)
    weight_lanes = -(-weight_cols.shape[1] // 128)
    weight_cols = jnp.pad(weight_cols, ((0, 0), (0, weight_lanes * 128 - weight_cols.shape[1])))
    weight_block = weight_cols.reshape(local_rows * weight_lanes, 128)
    weight_block = jnp.pad(weight_block, ((0, -weight_block.shape[0] % 16), (0, 0)))
    block = jnp.concatenate([normed.reshape(local_rows * lanes, 128), weight_block], axis=0)
    gate_up = dequantize(gate_up_codes[0], gate_up_scales[0])
    down_proj = dequantize(down_codes[0], down_scales[0])
    half_width = down_proj.shape[0]
    gathered = gather_blocks(block, 2)
    all_rows = shards * local_rows
    flat_rows = gathered[:, : local_rows * lanes].reshape(all_rows, feature_width)
    weight_all = gathered[
        :, local_rows * lanes : local_rows * lanes + local_rows * weight_lanes
    ].reshape(all_rows, weight_lanes * 128)
    column = jnp.arange(weight_lanes * 128, dtype=jnp.int32) % experts_all
    in_use = jnp.arange(weight_lanes * 128, dtype=jnp.int32) < 2 * experts_all
    is_mine = jnp.logical_and(column == device // 2, in_use)
    row_weight = jnp.sum(
        jnp.where(is_mine[None, :], weight_all.astype(jnp.float32), 0.0), axis=1, keepdims=True
    )
    projected_in = jnp.dot(flat_rows, gate_up, preferred_element_type=jnp.float32)
    activated = (jax.nn.silu(projected_in[:, :half_width]) * projected_in[:, half_width:]).astype(
        jnp.bfloat16
    )
    result = jnp.dot(activated, down_proj, preferred_element_type=jnp.float32)
    result = jnp.where(row_weight != 0.0, result * row_weight, 0.0).astype(jnp.bfloat16)
    expert_sum = scatter_sum(result.reshape(shards, local_rows * lanes, 128), 3).reshape(
        local_rows, feature_width
    )
    layer_out = (mixed_rows + expert_sum).astype(jnp.bfloat16)
    return (attention_out, layer_out)


def solution(mesh):
    return jax.shard_map(
        local,
        mesh=mesh,
        in_specs=(
            P(("replica", "ctx"), None),
            P(("replica", "ctx"), None),
            P(("replica", "ctx"), None),
            P("replica", "ctx", None),
            P("replica", "ctx", None),
            P("replica"),
            P("replica"),
            P(("replica", "ctx"), None),
            P("ctx", None),
            P(),
            P(("replica", "ctx"), None),
            P(("replica", "ctx"), None),
            P("ctx", None, None),
            P("ctx", None, None),
            P("ctx", None, None),
            P("ctx", None, None),
        ),
        out_specs=(P(("replica", "ctx"), None), P(("replica", "ctx"), None)),
        check_vma=False,
    )
```

profile of v0, /device:TPU:0, one launch (start us, length us, event | category | flops | bytes accessed | tf_op | source)
XLA Modules:
  0.0 166.3 jit_solution(10204794849153150938)
XLA Ops:
  1.7 1.3 gather_fusion
  3.0 1.3 gather_fusion.1
  4.4 4.1 %collective-permute-start = (bf16[1,1,32,512]{3,2,1,0:T(8,128)(2,1)S(1)}, bf16[1,1,32,512]{3,2,1,0:T(8,128)(2,1)S(1)}, u32[]{:S(2)}, u32[]{:S(2)}) collective-permute-start(bf16[1,1,32,512]{3,2,1,0:T(8,128)(2,1)S(1)} %fusion.39), channel_id=1, source_target_pairs={{0,16},{1,17},{2,18},{3,19},{4,20},{5,21},{6,22},{7,23},{8,24},{9,... | collective-permute-start | bytes 98312 | tf_op jit(solution)/shard_map/ppermute | solution.py:19
  12.6 8.8 %copy.128 = bf16[1,4096,768]{1,2,0:T(8,128)(2,1)} copy(bf16[1,4096,768]{2,1,0:T(8,128)(2,1)} %param.30) | data formatting | bytes 12582912 | tf_op args[12]
  22.4 7.4 %fusion = bf16[4096,6,128]{0,2,1:T(8,128)(2,1)} fusion(bf16[4096,6,128]{0,2,1:T(8,128)(2,1)} %bitcast.223, f32[4096,6]{0,1:T(8,128)S(1)} %bitcast.233), kind=kLoop, calls=%fused_computation.3 | loop fusion | flops 9437184 | bytes 12681216 | tf_op jit(solution)/shard_map/convert_element_type | solution.py:26
  29.8 1.6 collective-permute-start.2
  31.4 3.0 %collective-permute-done.2 = bf16[8,4096]{1,0:T(8,128)(2,1)S(1)} collective-permute-done((bf16[8,4096]{1,0:T(8,128)(2,1)S(1)}, bf16[8,4096]{1,0:T(8,128)(2,1)S(1)}, u32[]{:S(2)}, u32[]{:S(2)}) %collective-permute-start.2) | collective-permute-done | bytes 65568 | tf_op jit(solution)/shard_map/ppermute | solution.py:19
  34.4 1.6 collective-permute-start.3
  36.0 3.5 %collective-permute-done.3 = bf16[16,4096]{1,0:T(8,128)(2,1)S(1)} collective-permute-done((bf16[16,4096]{1,0:T(8,128)(2,1)S(1)}, bf16[16,4096]{1,0:T(8,128)(2,1)S(1)}, u32[]{:S(2)}, u32[]{:S(2)}) %collective-permute-start.3) | collective-permute-done | bytes 131104 | tf_op jit(solution)/shard_map/ppermute | solution.py:19
  39.6 1.6 collective-permute-start.4
  41.6 5.1 %collective-permute-done.4 = bf16[32,4096]{1,0:T(8,128)(2,1)S(1)} collective-permute-done((bf16[32,4096]{1,0:T(8,128)(2,1)S(1)}, bf16[32,4096]{1,0:T(8,128)(2,1)S(1)}, u32[]{:S(2)}, u32[]{:S(2)}) %collective-permute-start.4) | collective-permute-done | bytes 262176 | tf_op jit(solution)/shard_map/ppermute | solution.py:19
  48.3 1.6 collective-permute-start.13
  50.4 1.8 %multiply_reduce_fusion = f32[64,2,16,128]{3,0,2,1:T(8,128)S(1)} fusion(f32[64,2,16,2]{0,2,3,1:T(8,128)S(1)} %get-tuple-element.43, f32[64,2,16,2]{0,2,3,1:T(8,128)S(1)} %get-tuple-element.55, f32[1,64,2,16,2,32]{1,5,3,4,2,0:T(8,128)S(1)} %get-tuple-element.64, f32[64,2,16,2]{0,2,3,1:T(8,128)S(1)} %get-tuple-element.63, ...), kind=kOutput, calls=%fused_computation.13 | convolution fusion | flops 36306944 | bytes 1654848 | tf_op jit(solution)/shard_map/brgqst,bstgd->brgqsd/dot_general | solution.py:41
  52.4 1.6 collective-permute-start.6
  54.0 1.6 collective-permute-start.7
  56.2 1.5 collective-permute-done.7
  57.7 1.5 collective-permute-done.14
  59.3 1.6 collective-permute-start.9
  61.4 2.4 %collective-permute-done.6 = f32[32,32,128]{2,0,1:T(8,128)S(1)} collective-permute-done((f32[32,32,128]{2,0,1:T(8,128)S(1)}, f32[32,32,128]{2,0,1:T(8,128)S(1)}, u32[]{:S(2)}, u32[]{:S(2)}) %collective-permute-start.6) | collective-permute-done | bytes 524320 | tf_op jit(solution)/shard_map/ppermute | solution.py:19
  64.2 1.6 collective-permute-start.8
  66.1 4.6 %collective-permute-done.8 = f32[16,32,128]{2,1,0:T(8,128)S(1)} collective-permute-done((f32[16,32,128]{2,1,0:T(8,128)S(1)}, f32[16,32,128]{2,1,0:T(8,128)S(1)}, u32[]{:S(2)}, u32[]{:S(2)}) %collective-permute-start.8) | collective-permute-done | bytes 262176 | tf_op jit(solution)/shard_map/ppermute | solution.py:19
  70.9 1.6 collective-permute-start.10
  73.0 3.0 %collective-permute-done.10 = f32[8,32,128]{2,1,0:T(8,128)S(1)} collective-permute-done((f32[8,32,128]{2,1,0:T(8,128)S(1)}, f32[8,32,128]{2,1,0:T(8,128)S(1)}, u32[]{:S(2)}, u32[]{:S(2)}) %collective-permute-start.10) | collective-permute-done | bytes 131104 | tf_op jit(solution)/shard_map/ppermute | solution.py:19
  78.2 4.0 %all-to-all-start = ((bf16[4,32,128]{2,0,1:T(4,128)(2,1)}), bf16[4,32,128]{2,0,1:T(4,128)(2,1)S(1)}, u32[]{:S(2)}, u32[]{:S(2)}) async-start(bf16[4,32,128]{2,0,1:T(4,128)(2,1)} %copy.127), calls=%async_computation | async-start | bytes 65536 | tf_op jit(solution)/shard_map/all_to_all | solution.py:332
  82.2 7.1 %all-to-all-done = bf16[4,32,128]{2,0,1:T(4,128)(2,1)S(1)} async-done(((bf16[4,32,128]{2,0,1:T(4,128)(2,1)}), bf16[4,32,128]{2,0,1:T(4,128)(2,1)S(1)}, u32[]{:S(2)}, u32[]{:S(2)}) %all-to-all-start) | async-done | bytes 32800 | tf_op jit(solution)/shard_map/all_to_all | solution.py:332
  91.0 18.8 %scatter_sum.2 = f32[128,128]{1,0:T(8,128)} custom-call(bf16[32,128,128]{2,1,0:T(8,128)(2,1)} %reshape.322.refs_0_), custom_call_target="tpu_custom_call" | custom-call | tf_op jit(solution)/shard_map/scatter_sum/pallas_call | solution.py:218
  111.6 19.5 %gather_blocks.1 = bf16[32,144,128]{2,1,0:T(8,128)(2,1)} custom-call(bf16[144,128]{1,0:T(8,128)(2,1)} %fusion.37.refs_0_), custom_call_target="tpu_custom_call" | custom-call | tf_op jit(solution)/shard_map/gather_blocks/pallas_call | solution.py:144
  134.0 5.0 %fusion.84 = f32[128,768]{1,0:T(8,128)S(1)} fusion(bf16[128,4096]{1,0:T(8,128)(2,1)S(1)} %reshape.325, bf16[4096,768]{0,1:T(8,128)(2,1)} %bitcast.224), kind=kOutput, calls=%fused_computation.167 | convolution fusion | flops 805306368 | bytes 7733248 | tf_op jit(solution)/shard_map/dot_general | solution.py:367
  139.1 1.8 %broadcast_in_dim.123 = f32[384,32,128]{2,1,0:T(8,128)S(1)} broadcast(f32[384,32]{1,0:T(8,128)S(1)} %bitcast.232), dimensions={0,1} | broadcast | bytes 6340608 | tf_op jit(solution)/shard_map/broadcast_in_dim | solution.py:25
  141.0 4.0 %fusion.3 = bf16[128,4096]{1,0:T(8,128)(2,1)S(1)} fusion(f32[48,8,32,128]{3,2,1,0:T(8,128)S(1)} %bitcast.225, bf16[1,384,4096]{2,1,0:T(8,128)(2,1)S(1)} %copy-done.1, f32[128]{0:T(128)S(1)} %reduce_sum.62, pred[128]{0:T(512)(128)(4,1)S(1)} %broadcast_compare_fusion, f32[128,768]{1,0:T(8,128)S(1)} %fusion.84), kind=kOutput, calls=%fused_computation.8 | convolution fusion | flops 409239552 | bytes 10879616 | tf_op jit(solution)/shard_map/dot_general | solution.py:371
  145.0 1.3 reshape.329.refs_0_
  146.3 18.5 %scatter_sum.3 = f32[128,128]{1,0:T(8,128)} custom-call(bf16[32,128,128]{2,1,0:T(8,128)(2,1)} %reshape.329.refs_0_), custom_call_target="tpu_custom_call" | custom-call | tf_op jit(solution)/shard_map/scatter_sum/pallas_call | solution.py:218
  (124 shorter events, 20.3 us)
Async XLA Ops:
  0.6 88.7 %copy-start = (bf16[128,4096]{1,0:T(8,128)(2,1)S(1)}, bf16[128,4096]{1,0:T(8,128)(2,1)}, u32[]{:S(2)}) copy-start(bf16[128,4096]{1,0:T(8,128)(2,1)} %param.26) | copy-start | bytes 3145732
  4.4 27.0 %collective-permute-start = (bf16[1,1,32,512]{3,2,1,0:T(8,128)(2,1)S(1)}, bf16[1,1,32,512]{3,2,1,0:T(8,128)(2,1)S(1)}, u32[]{:S(2)}, u32[]{:S(2)}) collective-permute-start(bf16[1,1,32,512]{3,2,1,0:T(8,128)(2,1)S(1)} %fusion.39), channel_id=1, source_target_pairs={{0,16},{1,17},{2,18},{3,19},{4,20},{5,21},{6,22},{7,23},{8,24},{9,... | collective-permute-start | bytes 98312 | tf_op jit(solution)/shard_map/ppermute | solution.py:19
  8.5 21.2 %collective-permute-start.1 = (bf16[4,4096]{1,0:T(4,128)(2,1)}, bf16[4,4096]{1,0:T(4,128)(2,1)S(1)}, u32[]{:S(2)}, u32[]{:S(2)}) collective-permute-start(bf16[4,4096]{1,0:T(4,128)(2,1)} %param.18), channel_id=1, source_target_pairs={{0,1},{1,0},{2,3},{3,2},{4,5},{5,4},{6,7},{7,6},{8,9},{9,8},{10,11... | collective-permute-start | bytes 98312 | tf_op jit(solution)/shard_map/ppermute | solution.py:19
  12.5 8.8 %copy-start.5 = (f32[1,32,6]{1,0,2:T(1,128)S(1)}, f32[1,32,6]{1,0,2:T(1,128)}, u32[]{:S(2)}) copy-start(f32[1,32,6]{1,0,2:T(1,128)} %param.31) | copy-start | bytes 2308
  12.5 9.7 %copy-start.6 = (f32[4,8]{1,0:T(4,128)S(1)}, f32[4,8]{1,0:T(4,128)}, u32[]{:S(2)}) copy-start(f32[4,8]{1,0:T(4,128)} %param.29) | copy-start | bytes 388
  12.6 9.7 %copy-start.7 = (s32[4,8]{1,0:T(4,128)S(1)}, s32[4,8]{1,0:T(4,128)}, u32[]{:S(2)}) copy-start(s32[4,8]{1,0:T(4,128)} %param.28) | copy-start | bytes 388
  22.4 7.4 %copy-start.3 = (bf16[4,4096]{1,0:T(4,128)(2,1)S(1)}, bf16[4,4096]{1,0:T(4,128)(2,1)}, u32[]{:S(2)}) copy-start(bf16[4,4096]{1,0:T(4,128)(2,1)} %param.18) | copy-start | bytes 98308
  29.8 4.6 %collective-permute-start.2 = (bf16[8,4096]{1,0:T(8,128)(2,1)S(1)}, bf16[8,4096]{1,0:T(8,128)(2,1)S(1)}, u32[]{:S(2)}, u32[]{:S(2)}) collective-permute-start(bf16[8,4096]{1,0:T(8,128)(2,1)S(1)} %maximum_select_fusion.6), channel_id=1, source_target_pairs={{0,2},{1,3},{2,0},{3,1},{4,6},{5,7},{6,4},{7,5},{8,10},{9,11},{10,... | collective-permute-start | bytes 196616 | tf_op jit(solution)/shard_map/ppermute | solution.py:19
  34.4 5.1 %collective-permute-start.3 = (bf16[16,4096]{1,0:T(8,128)(2,1)S(1)}, bf16[16,4096]{1,0:T(8,128)(2,1)S(1)}, u32[]{:S(2)}, u32[]{:S(2)}) collective-permute-start(bf16[16,4096]{1,0:T(8,128)(2,1)S(1)} %maximum_select_fusion.4), channel_id=1, source_target_pairs={{0,4},{1,5},{2,6},{3,7},{4,0},{5,1},{6,2},{7,3},{8,12},{9,13},{10,... | collective-permute-start | bytes 393224 | tf_op jit(solution)/shard_map/ppermute | solution.py:19
  39.6 7.1 %collective-permute-start.4 = (bf16[32,4096]{1,0:T(8,128)(2,1)S(1)}, bf16[32,4096]{1,0:T(8,128)(2,1)S(1)}, u32[]{:S(2)}, u32[]{:S(2)}) collective-permute-start(bf16[32,4096]{1,0:T(8,128)(2,1)S(1)} %maximum_select_fusion.2), channel_id=1, source_target_pairs={{0,8},{1,9},{2,10},{3,11},{4,12},{5,13},{6,14},{7,15},{8,0},{9,1},... | collective-permute-start | bytes 786440 | tf_op jit(solution)/shard_map/ppermute | solution.py:19
  48.3 5.7 %collective-permute-start.13 = (f32[32,32]{1,0:T(8,128)S(1)}, f32[32,32]{1,0:T(8,128)S(1)}, u32[]{:S(2)}, u32[]{:S(2)}) collective-permute-start(f32[32,32]{1,0:T(8,128)S(1)} %bitcast.253), channel_id=1, source_target_pairs={{0,8},{1,9},{2,10},{3,11},{4,12},{5,13},{6,14},{7,15},{8,0},{9,1},... | collective-permute-start | bytes 12296 | tf_op jit(solution)/shard_map/ppermute | solution.py:19
  49.9 4.0 %collective-permute-start.5 = (f32[32,32]{1,0:T(8,128)S(1)}, f32[32,32]{1,0:T(8,128)S(1)}, u32[]{:S(2)}, u32[]{:S(2)}) collective-permute-start(f32[32,32]{1,0:T(8,128)S(1)} %bitcast.254), channel_id=1, source_target_pairs={{0,8},{1,9},{2,10},{3,11},{4,12},{5,13},{6,14},{7,15},{8,0},{9,1},... | collective-permute-start | bytes 12296 | tf_op jit(solution)/shard_map/ppermute | solution.py:19
  52.1 13.8 %copy-start.8 = (bf16[4,256]{1,0:T(4,128)(2,1)S(1)}, bf16[4,256]{1,0:T(4,128)(2,1)}, u32[]{:S(2)}) copy-start(bf16[4,256]{1,0:T(4,128)(2,1)} %param.20) | copy-start | bytes 6148
  52.1 13.8 %copy-start.9 = (f32[1,3,32]{2,0,1:T(1,128)S(1)}, f32[1,3,32]{2,0,1:T(1,128)}, u32[]{:S(2)}) copy-start(f32[1,3,32]{2,0,1:T(1,128)} %param.33) | copy-start | bytes 1156
  52.4 11.4 %collective-permute-start.6 = (f32[32,32,128]{2,0,1:T(8,128)S(1)}, f32[32,32,128]{2,0,1:T(8,128)S(1)}, u32[]{:S(2)}, u32[]{:S(2)}) collective-permute-start(f32[32,32,128]{2,0,1:T(8,128)S(1)} %dynamic-slice_bitcast_fusion), channel_id=1, source_target_pairs={{0,8},{1,9},{2,10},{3,11},{4,12},{5,13},{6,14},{7,15},{8,0},{9,1},... | collective-permute-start | bytes 1572872 | tf_op jit(solution)/shard_map/ppermute | solution.py:19
  54.0 3.7 %collective-permute-start.7 = (f32[16,32]{1,0:T(8,128)S(1)}, f32[16,32]{1,0:T(8,128)S(1)}, u32[]{:S(2)}, u32[]{:S(2)}) collective-permute-start(f32[16,32]{1,0:T(8,128)S(1)} %dynamic-slice_bitcast_fusion.4), channel_id=1, source_target_pairs={{0,4},{1,5},{2,6},{3,7},{4,0},{5,1},{6,2},{7,3},{8,12},{9,13},{10,... | collective-permute-start | bytes 6152 | tf_op jit(solution)/shard_map/ppermute | solution.py:19
  55.6 3.7 %collective-permute-start.14 = (f32[16,32]{1,0:T(8,128)S(1)}, f32[16,32]{1,0:T(8,128)S(1)}, u32[]{:S(2)}, u32[]{:S(2)}) collective-permute-start(f32[16,32]{1,0:T(8,128)S(1)} %dynamic-slice_bitcast_fusion.3), channel_id=1, source_target_pairs={{0,4},{1,5},{2,6},{3,7},{4,0},{5,1},{6,2},{7,3},{8,12},{9,13},{10,... | collective-permute-start | bytes 6152 | tf_op jit(solution)/shard_map/ppermute | solution.py:19
  59.3 6.8 %collective-permute-start.9 = (f32[8,32]{1,0:T(8,128)S(1)}, f32[8,32]{1,0:T(8,128)S(1)}, u32[]{:S(2)}, u32[]{:S(2)}) collective-permute-start(f32[8,32]{1,0:T(8,128)S(1)} %fusion.48), channel_id=1, source_target_pairs={{0,2},{1,3},{2,0},{3,1},{4,6},{5,7},{6,4},{7,5},{8,10},{9,11},{10,... | collective-permute-start | bytes 3080 | tf_op jit(solution)/shard_map/ppermute | solution.py:19
  60.8 5.2 %collective-permute-start.15 = (f32[8,32]{1,0:T(8,128)S(1)}, f32[8,32]{1,0:T(8,128)S(1)}, u32[]{:S(2)}, u32[]{:S(2)}) collective-permute-start(f32[8,32]{1,0:T(8,128)S(1)} %fusion.52), channel_id=1, source_target_pairs={{0,2},{1,3},{2,0},{3,1},{4,6},{5,7},{6,4},{7,5},{8,10},{9,11},{10,... | collective-permute-start | bytes 3080 | tf_op jit(solution)/shard_map/ppermute | solution.py:19
  64.2 6.4 %collective-permute-start.8 = (f32[16,32,128]{2,1,0:T(8,128)S(1)}, f32[16,32,128]{2,1,0:T(8,128)S(1)}, u32[]{:S(2)}, u32[]{:S(2)}) collective-permute-start(f32[16,32,128]{2,1,0:T(8,128)S(1)} %bitcast.240), channel_id=1, source_target_pairs={{0,4},{1,5},{2,6},{3,7},{4,0},{5,1},{6,2},{7,3},{8,12},{9,13},{10,... | collective-permute-start | bytes 786440 | tf_op jit(solution)/shard_map/ppermute | solution.py:19
  70.9 5.0 %collective-permute-start.10 = (f32[8,32,128]{2,1,0:T(8,128)S(1)}, f32[8,32,128]{2,1,0:T(8,128)S(1)}, u32[]{:S(2)}, u32[]{:S(2)}) collective-permute-start(f32[8,32,128]{2,1,0:T(8,128)S(1)} %dynamic-slice_bitcast_fusion.1), channel_id=1, source_target_pairs={{0,2},{1,3},{2,0},{3,1},{4,6},{5,7},{6,4},{7,5},{8,10},{9,11},{10,... | collective-permute-start | bytes 393224 | tf_op jit(solution)/shard_map/ppermute | solution.py:19
  72.5 3.7 %collective-permute-start.11 = (f32[4,32]{1,0:T(4,128)S(1)}, f32[4,32]{1,0:T(4,128)S(1)}, u32[]{:S(2)}, u32[]{:S(2)}) collective-permute-start(f32[4,32]{1,0:T(4,128)S(1)} %fusion.58), channel_id=1, source_target_pairs={{0,1},{1,0},{2,3},{3,2},{4,5},{5,4},{6,7},{7,6},{8,9},{9,8},{10,11... | collective-permute-start | bytes 1544 | tf_op jit(solution)/shard_map/ppermute | solution.py:19
  72.5 3.7 %collective-permute-start.16 = (f32[4,32]{1,0:T(4,128)S(1)}, f32[4,32]{1,0:T(4,128)S(1)}, u32[]{:S(2)}, u32[]{:S(2)}) collective-permute-start(f32[4,32]{1,0:T(4,128)S(1)} %fusion.64), channel_id=1, source_target_pairs={{0,1},{1,0},{2,3},{3,2},{4,5},{5,4},{6,7},{7,6},{8,9},{9,8},{10,11... | collective-permute-start | bytes 1544 | tf_op jit(solution)/shard_map/ppermute | solution.py:19
  75.9 34.8 %copy-start.2 = (bf16[4,4096]{1,0:T(4,128)(2,1)S(1)}, bf16[4,4096]{1,0:T(4,128)(2,1)}, u32[]{:S(2)}) copy-start(bf16[4,4096]{1,0:T(4,128)(2,1)} %param.25) | copy-start | bytes 98308
  75.9 34.9 %copy-start.4 = (f32[4096]{0:T(1024)S(1)}, f32[4096]{0:T(1024)}, u32[]{:S(2)}) copy-start(f32[4096]{0:T(1024)} %param.27) | copy-start | bytes 49156
  76.1 1.3 collective-permute-start.12
  78.2 11.1 %all-to-all-start = ((bf16[4,32,128]{2,0,1:T(4,128)(2,1)}), bf16[4,32,128]{2,0,1:T(4,128)(2,1)S(1)}, u32[]{:S(2)}, u32[]{:S(2)}) async-start(bf16[4,32,128]{2,0,1:T(4,128)(2,1)} %copy.127), calls=%async_computation | async-start | bytes 65536 | tf_op jit(solution)/shard_map/all_to_all | solution.py:332
  139.1 1.9 %copy-start.1 = (bf16[1,384,4096]{2,1,0:T(8,128)(2,1)S(1)}, bf16[1,384,4096]{2,1,0:T(8,128)(2,1)}, u32[]{:S(2)}) copy-start(bf16[1,384,4096]{2,1,0:T(8,128)(2,1)} %param.32) | copy-start | bytes 9437188
where the time goes:
time: 167 us; the launch traced here: 166 us
  Pallas kernels  56.8 us (34%)
  waiting for transfers between devices  32.8 us (20%)
  local copies, waits for them, and re-layouts  25.8 us (15%)
  starting transfers between devices  24.5 us (15%)
  matrix products  12 us (7%)
  other arithmetic  11.9 us (7%)
  between operations  2.56 us (2%)
    pallas_call x2, Pallas kernels, scatter_sum(): pl.pallas_call(lambda *refs: scatter_kernel(bits, *refs), out_shape=jax.S...  37.3 us
    ppermute x17, waiting for transfers between devices, swapped(): lax.ppermute(value, axis, [(i, i ^ 1 << distance) for i in range(lax.axis...  25.8 us
    ppermute x17, starting transfers between devices, swapped(): lax.ppermute(value, axis, [(i, i ^ 1 << distance) for i in range(lax.axis...  20.4 us
    pallas_call x1, Pallas kernels, gather_blocks(): pl.pallas_call(lambda *refs: gather_kernel(bits, *refs), out_shape=jax.Sh...  19.5 us
    unnamed x28, local copies, waits for them, and re-layouts  9.92 us
    convert_element_type x1, other arithmetic, dequantize(): return (code_values.astype(jnp.float32) * spread).astype(jnp.bfloat16)  7.36 us
    all_to_all x1, waiting for transfers between devices, local(): lax.all_to_all(attended, 'ctx', split_axis=1, concat_axis=0, tiled=True)  7.06 us
    dot_general x1, matrix products, local(): jnp.dot(flat_rows, gate_up, preferred_element_type=jnp.float32)  4.99 us
  transfers between devices with their start and end apart: 18, of which 10 were waited for; matrix products, arithmetic and copies ran while one was open for 14% of the time, Pallas kernels for 0%

commit v1 on v0

--- a/solution.py
+++ b/solution.py
@@ -231,7 +231,7 @@
     )(blocks)
 
 
-def local(
+def staged_layer(
     queries,
     own_key,
     own_value,
@@ -377,6 +377,558 @@
     return (attention_out, layer_out)
 
 
+def remote(source, target, send_sem, recv_sem, device):
+    copy = pltpu.make_async_remote_copy(
+        src_ref=source,
+        dst_ref=target,
+        send_sem=send_sem,
+        recv_sem=recv_sem,
+        device_id={"ctx": device},
+        device_id_type=pl.DeviceIdType.MESH,
+    )
+    copy.start()
+    return copy
+
+
+class Place:
+    def __init__(self, shards):
+        self.shards = shards
+        self.bits = shards.bit_length() - 1
+        self.column = shards // 8
+        self.me = lax.axis_index("ctx")
+        self.known = {0: self.me}
+
+    def peer(self, pattern):
+        if pattern not in self.known:
+            self.known[pattern] = flipped(self.me, pattern, self.bits)
+        return self.known[pattern]
+
+    def peers(self):
+        return [k * 8 for k in range(1, self.column)] + [2, 4, 6, 1]
+
+    def greet(self):
+        barrier = pltpu.get_barrier_semaphore()
+        for pattern in self.peers():
+            pl.semaphore_signal(
+                barrier,
+                inc=1,
+                device_id={"ctx": self.peer(pattern)},
+                device_id_type=pl.DeviceIdType.MESH,
+            )
+
+    def met(self):
+        pl.semaphore_wait(pltpu.get_barrier_semaphore(), len(self.peers()))
+
+
+def spread(place, column_source, own, buffer, sems, on_column, on_plane, on_core, filler):
+    send_sem, recv_sem = sems
+    copies = {}
+
+    def post(source, block, slot, towards):
+        copies[slot] = remote(
+            source,
+            buffer.at[place.peer(block)],
+            send_sem.at[slot],
+            recv_sem.at[slot],
+            place.peer(towards),
+        )
+
+    def forward(k):
+        source = own if k == 0 else buffer.at[place.peer(k * 8)]
+        for plane in (6, 2, 4):
+            post(source, k * 8, k * 8 + plane, plane)
+        post(source, k * 8, k * 8 + 1, 1)
+
+    for k in reversed(range(1, place.column)):
+        post(column_source(k), 0, k * 8, k * 8)
+    forward(0)
+    on_column(0)
+    for k in range(1, place.column):
+        copies[k * 8].wait_recv()
+        forward(k)
+        on_column(k)
+    filler()
+    for k in range(place.column):
+        on_plane(k * 8)
+        for plane in (2, 4, 6):
+            slot = k * 8 + plane
+            copies[slot].wait_recv()
+            post(buffer.at[place.peer(slot)], slot, slot + 1, 1)
+            on_plane(slot)
+    for slot in range(0, place.shards, 2):
+        copies[slot + 1].wait_recv()
+        on_core(slot + 1)
+    return list(copies.values())
+
+
+def collect(place, values, size, boxes, sems, filler):
+    send_sem, recv_sem = sems
+    core_out, core_in, plane_out, plane_in, column_out, column_in = boxes
+    kind = core_out.dtype
+    copies = {}
+    chips = place.shards // 2
+
+    def held(pattern):
+        start = pl.multiple_of(place.peer(pattern) * size, size)
+        return values[pl.ds(start, size), :]
+
+    order = [k * 4 + p for k in reversed(range(place.column)) for p in (3, 1, 2)]
+    order = order + [k * 4 for k in reversed(range(place.column))]
+    for chip in order:
+        core_out[chip] = held(chip * 2 + 1).astype(kind)
+        copies[chip] = remote(
+            core_out.at[chip], core_in.at[chip], send_sem.at[chip], recv_sem.at[chip], place.peer(1)
+        )
+
+    def on_chip(chip):
+        copies[chip].wait_recv()
+        return held(chip * 2) + core_in[chip].astype(jnp.float32)
+
+    for k in reversed(range(place.column)):
+        for p in (3, 1, 2):
+            chip = k * 4 + p
+            plane_out[chip] = on_chip(chip).astype(kind)
+            copies[chips + chip] = remote(
+                plane_out.at[chip],
+                plane_in.at[chip],
+                send_sem.at[chips + chip],
+                recv_sem.at[chips + chip],
+                place.peer(p * 2),
+            )
+    filler()
+
+    def on_plane(k):
+        total = on_chip(k * 4)
+        for p in (1, 2, 3):
+            copies[chips + k * 4 + p].wait_recv()
+            total = total + plane_in[k * 4 + p].astype(jnp.float32)
+        return total
+
+    for k in reversed(range(1, place.column)):
+        column_out[k] = on_plane(k).astype(kind)
+        copies[chips + k * 4] = remote(
+            column_out.at[k],
+            column_in.at[k],
+            send_sem.at[chips + k * 4],
+            recv_sem.at[chips + k * 4],
+            place.peer(k * 8),
+        )
+    total = on_plane(0)
+    for k in range(1, place.column):
+        copies[chips + k * 4].wait_recv()
+        total = total + column_in[k].astype(jnp.float32)
+    return total, list(copies.values())
+
+
+def layer_kernel(
+    shards,
+    per_block,
+    prefix_ref,
+    length_ref,
+    gate_scale_ref,
+    down_scale_ref,
+    queries_ref,
+    own_key_ref,
+    own_value_ref,
+    keys_ref,
+    values_ref,
+    hidden_ref,
+    gain_ref,
+    ids_ref,
+    route_ref,
+    w_out_hbm,
+    gate_hbm,
+    down_hbm,
+    attention_ref,
+    layer_ref,
+    w_out_ref,
+    gate_ref,
+    down_ref,
+    load_sem,
+    stage,
+    q_send,
+    q_column,
+    q_plane,
+    q_all,
+    q_wide,
+    kv_send,
+    kv_all,
+    own_wide,
+    attended,
+    partial,
+    mixed_ref,
+    normed_send,
+    normed_all,
+    rows_wide,
+    rows_ref,
+    *boxes_and_sems,
+):
+    first_boxes, second_boxes = boxes_and_sems[0:6], boxes_and_sems[6:12]
+    sems = boxes_and_sems[12:]
+    q_sems, kv_sems, first_sems, row_sems, second_sems = [sems[2 * i : 2 * i + 2] for i in range(5)]
+    place = Place(shards)
+    me = place.me
+    local_rows, width = queries_ref.shape
+    lanes = width // 128
+    size = local_rows * lanes
+    prefixes, positions, _ = keys_ref.shape
+    blocks = shards // per_block
+    span = blocks * positions
+    key_groups = own_key_ref.shape[1] // HD
+    per_group = shards // key_groups
+    score_scale = 1.0 / math.sqrt(HD)
+    f32 = jnp.float32
+
+    loads = []
+    for i, (source, target) in enumerate(
+        ((w_out_hbm, w_out_ref), (gate_hbm.at[0], gate_ref), (down_hbm.at[0], down_ref))
+    ):
+        load = pltpu.make_async_copy(source, target, load_sem.at[i])
+        load.start()
+        loads.append(load)
+    place.greet()
+
+    lengths = []
+    for b in range(blocks):
+        prefix = prefix_ref[b * per_block * local_rows]
+        length = length_ref[0]
+        for p in range(1, prefixes):
+            length = jnp.where(prefix == p, length_ref[p], length)
+        lengths.append(length)
+        prefix_of = jnp.full((positions, keys_ref.shape[2]), prefix, jnp.int32)
+        for which, ref in enumerate((keys_ref, values_ref)):
+            chosen = ref[0].astype(f32)
+            for p in range(1, prefixes):
+                chosen = jnp.where(prefix_of == p, ref[p].astype(f32), chosen)
+            at = which * span + b * positions
+            for g in range(key_groups):
+                kv_send[g, at : at + positions, :] = chosen[:, g * HD : (g + 1) * HD].astype(
+                    jnp.bfloat16
+                )
+    for g in range(key_groups):
+        cut = slice(g * HD, (g + 1) * HD)
+        stage[0:16, :] = jnp.zeros((16, HD), f32)
+        stage[0:local_rows, :] = own_key_ref[:, cut].astype(f32)
+        stage[8 : 8 + local_rows, :] = own_value_ref[:, cut].astype(f32)
+        kv_send[g, 2 * span : 2 * span + 16, :] = stage[0:16, :].astype(jnp.bfloat16)
+    lane = lax.broadcasted_iota(jnp.int32, (local_rows, 128), 1)
+    for expert in range(shards // 2):
+        weight = jnp.sum(
+            jnp.where(ids_ref[...] == expert, route_ref[...], 0.0), axis=1, keepdims=True
+        )
+        weight = jnp.broadcast_to(weight, (local_rows, 128))
+        coarse = weight.astype(jnp.bfloat16).astype(f32)
+        both = jnp.where(lane < 64, coarse, weight - coarse)
+        for d in (2 * expert, 2 * expert + 1):
+            stage[8 * d : 8 * d + local_rows, :] = queries_ref[:, d * HD : (d + 1) * HD].astype(f32)
+            stage[8 * d + local_rows : 8 * d + 2 * local_rows, :] = both
+    q_send[...] = stage[...].reshape(shards, 8, 128).astype(jnp.bfloat16)
+    place.met()
+
+    q_copies = {}
+
+    def q_post(source, target, slot, towards):
+        q_copies[slot] = remote(
+            source, target, q_sems[0].at[slot], q_sems[1].at[slot], place.peer(towards)
+        )
+
+    def q_blocks(slot, start, count):
+        k, plane = slot // 8, slot % 8 // 2
+        if plane:
+            return q_plane.at[k * 4 + plane, pl.ds(start % 2, count)]
+        if k:
+            return q_column.at[k, pl.ds(start % 8, count)]
+        return q_send.at[pl.ds(start, count)]
+
+    for k in reversed(range(1, place.column)):
+        q_post(q_send.at[pl.ds(place.peer(k * 8) // 8 * 8, 8)], q_column.at[k], k * 8, k * 8)
+
+    def q_on_column(k):
+        if k:
+            q_copies[k * 8].wait_recv()
+        for plane in (3, 1, 2):
+            start = place.peer(plane * 2) // 2 * 2
+            q_post(
+                q_blocks(k * 8, start, 2), q_plane.at[k * 4 + plane], k * 8 + plane * 2, plane * 2
+            )
+
+    def q_on_plane(slot):
+        if slot % 8:
+            q_copies[slot].wait_recv()
+        origin = place.peer(slot)
+        q_post(
+            q_blocks(slot, place.peer(1), 1), q_all.at[pl.ds(origin, 1)], slot + 1, 1
+        )
+        q_all[pl.ds(origin, 1)] = q_blocks(slot, me, 1)[...]
+
+    def q_on_core(slot):
+        q_copies[slot].wait_recv()
+
+    my_group = me // per_group
+
+    def dequantize_gate():
+        loads[1].wait()
+
+        def block_row(i, carry):
+            at = pl.ds(pl.multiple_of(i * 128, 128), 128)
+            for j in range(gate_ref.shape[1] // 128):
+                cut = slice(j * 128, (j + 1) * 128)
+                wide = gate_ref[at, cut].astype(f32) * gate_scale_ref[0, i, j]
+                gate_ref[at, cut] = wide.astype(jnp.bfloat16)
+            return carry
+
+        lax.fori_loop(0, gate_ref.shape[0] // 128, block_row, 0)
+
+    def dequantize_down():
+        loads[2].wait()
+
+        def block_column(j, carry):
+            at = pl.ds(pl.multiple_of(j * 128, 128), 128)
+            for i in range(down_ref.shape[0] // 128):
+                cut = slice(i * 128, (i + 1) * 128)
+                wide = down_ref[cut, at].astype(f32) * down_scale_ref[0, i, j]
+                down_ref[cut, at] = wide.astype(jnp.bfloat16)
+            return carry
+
+        lax.fori_loop(0, down_ref.shape[1] // 128, block_column, 0)
+
+    kv_all[pl.ds(me, 1)] = kv_send[pl.ds(my_group, 1)]
+    waits = spread(
+        place,
+        lambda k: kv_send.at[place.peer(k * 8) // per_group],
+        kv_send.at[my_group],
+        kv_all,
+        kv_sems,
+        q_on_column,
+        q_on_plane,
+        q_on_core,
+        dequantize_gate,
+    )
+
+    q_wide[...] = q_all[...].astype(f32).reshape(shards * 8, 128)
+    own_wide[...] = kv_all[:, 2 * span : 2 * span + 16, :].astype(f32).reshape(shards * 16, 128)
+    total_positions = shards * positions
+    position = lax.broadcasted_iota(jnp.int32, (1, total_positions), 1)
+
+    def picked(ref, start, count, stride):
+        return jnp.concatenate(
+            [ref[pl.ds(start + r, count, stride=stride), :] for r in range(local_rows)], axis=0
+        )
+
+    for b in range(blocks):
+        first = b * per_block
+        key_at, value_at = b * positions, span + b * positions
+        key = kv_all[:, key_at : key_at + positions, :].reshape(total_positions, HD)
+        value = kv_all[:, value_at : value_at + positions, :].reshape(total_positions, HD)
+        query = picked(q_wide, first * 8, per_block, 8)
+        own_k = picked(own_wide, first * 16, per_block, 16)
+        own_v = picked(own_wide, first * 16 + 8, per_block, 16)
+        scores = lax.dot_general(
+            query.astype(jnp.bfloat16), key, (((1,), (1,)), ((), ())), preferred_element_type=f32
+        )
+        is_valid = position < lengths[b]
+        scores = jnp.where(is_valid, scores * score_scale, NEG)
+        own_score = jnp.sum(query * own_k, axis=1, keepdims=True) * score_scale
+        top = jnp.maximum(jnp.max(scores, axis=1, keepdims=True), own_score)
+        weights = jnp.where(is_valid, jnp.exp(scores - top), 0.0)
+        own_weight = jnp.exp(own_score - top)
+        denominator = jnp.sum(weights, axis=1, keepdims=True) + own_weight
+        numerator = jnp.dot(weights.astype(jnp.bfloat16), value, preferred_element_type=f32)
+        result = (numerator + own_weight * own_v) / denominator
+        for r in range(local_rows):
+            attended[r * shards + first : r * shards + first + per_block, :] = result[
+                r * per_block : (r + 1) * per_block, :
+            ]
+
+    def scatter_rows(result, first_lane):
+        for i in range(result.shape[1] // 128):
+            for r in range(local_rows):
+                partial[pl.ds(r * lanes + first_lane + i, shards, stride=size), :] = result[
+                    r * shards : (r + 1) * shards, i * 128 : (i + 1) * 128
+                ]
+
+    loads[0].wait()
+    head_rows = attended[...].astype(jnp.bfloat16)
+    for i in range(0, width, 512):
+        scatter_rows(
+            jnp.dot(head_rows, w_out_ref[:, i : i + 512], preferred_element_type=f32), i // 128
+        )
+
+    projected, more = collect(place, partial, size, first_boxes, first_sems, dequantize_down)
+    waits = waits + more
+
+    for i in range(lanes):
+        mixed_ref[pl.ds(i, local_rows, stride=lanes), :] = hidden_ref[
+            :, i * 128 : (i + 1) * 128
+        ].astype(f32)
+    mixed = mixed_ref[...] + projected
+    mixed_ref[...] = mixed
+    grouped = mixed.reshape(local_rows, lanes, 128)
+    mean_square = (
+        jnp.sum(jnp.sum(grouped * grouped, axis=1, keepdims=True), axis=2, keepdims=True) / width
+    )
+    normed = grouped * lax.rsqrt(mean_square + EPSILON) * gain_ref[...][None]
+    normed_send[...] = normed.reshape(size, 128).astype(jnp.bfloat16)
+
+    def widen(slot):
+        at = pl.ds(pl.multiple_of(place.peer(slot) * size, size), size)
+        block = normed_all[place.peer(slot)] if slot else normed_send[...]
+        rows_wide[at, :] = block.astype(f32)
+
+    def write_attention():
+        for i in range(lanes):
+            attention_ref[:, i * 128 : (i + 1) * 128] = mixed_ref[
+                pl.ds(i, local_rows, stride=lanes), :
+            ].astype(jnp.bfloat16)
+
+    more = spread(
+        place,
+        lambda k: normed_send,
+        normed_send,
+        normed_all,
+        row_sems,
+        lambda k: None,
+        widen,
+        widen,
+        write_attention,
+    )
+    waits = waits + more
+    for i in range(lanes):
+        for r in range(local_rows):
+            rows_ref[r * shards : (r + 1) * shards, i * 128 : (i + 1) * 128] = rows_wide[
+                pl.ds(r * lanes + i, shards, stride=size), :
+            ].astype(jnp.bfloat16)
+    half = down_ref.shape[0]
+    projected_in = jnp.dot(rows_ref[...], gate_ref[...], preferred_element_type=f32)
+    split = picked(q_wide, local_rows, shards, 8)
+    weight = split[:, 0:1] + split[:, 64:65]
+    gate = projected_in[:, :half]
+    activated = gate / (1.0 + jnp.exp(-gate)) * projected_in[:, half:]
+    activated = jnp.where(weight != 0.0, activated * weight, 0.0).astype(jnp.bfloat16)
+    for i in range(0, width, 512):
+        scatter_rows(
+            jnp.dot(activated, down_ref[:, i : i + 512], preferred_element_type=f32), i // 128
+        )
+    expert_sum, more = collect(place, partial, size, second_boxes, second_sems, lambda: None)
+    waits = waits + more
+    mixed_ref[...] = mixed_ref[...] + expert_sum
+    for i in range(lanes):
+        layer_ref[:, i * 128 : (i + 1) * 128] = mixed_ref[
+            pl.ds(i, local_rows, stride=lanes), :
+        ].astype(jnp.bfloat16)
+    for copy in waits + list(q_copies.values()):
+        copy.wait_send()
+
+
+def fused_layer(
+    queries,
+    own_key,
+    own_value,
+    cache_keys,
+    cache_values,
+    prefix_of_row,
+    context_len,
+    hidden_in,
+    w_out,
+    norm_gain,
+    expert_ids,
+    route_weights,
+    gate_up_codes,
+    gate_up_scales,
+    down_codes,
+    down_scales,
+):
+    shards = lax.axis_size("ctx")
+    local_rows, width = queries.shape
+    lanes = width // 128
+    size = local_rows * lanes
+    span = shards * local_rows // CAND * cache_keys.shape[1]
+    column = shards // 8
+    bf16, f32 = jnp.bfloat16, jnp.float32
+    kv_rows = 2 * span + 16
+    boxes = [
+        pltpu.VMEM((count, size, 128), bf16)
+        for count in (shards // 2, shards // 2, shards // 2, shards // 2, column, column)
+    ]
+    smem = pl.BlockSpec(memory_space=pltpu.SMEM)
+    vmem = pl.BlockSpec(memory_space=pltpu.VMEM)
+    hbm = pl.BlockSpec(memory_space=pl.ANY)
+    out = jax.ShapeDtypeStruct((local_rows, width), bf16)
+    return pl.pallas_call(
+        lambda *refs: layer_kernel(shards, CAND // local_rows, *refs),
+        out_shape=(out, out),
+        in_specs=[smem] * 4 + [vmem] * 9 + [hbm] * 3,
+        out_specs=(vmem, vmem),
+        scratch_shapes=[
+            pltpu.VMEM(w_out.shape, bf16),
+            pltpu.VMEM(gate_up_codes.shape[1:], bf16),
+            pltpu.VMEM(down_codes.shape[1:], bf16),
+            pltpu.SemaphoreType.DMA((3,)),
+            pltpu.VMEM((shards * 8, 128), f32),
+            pltpu.VMEM((shards, 8, 128), bf16),
+            pltpu.VMEM((column, 8, 8, 128), bf16),
+            pltpu.VMEM((column * 4, 2, 8, 128), bf16),
+            pltpu.VMEM((shards, 8, 128), bf16),
+            pltpu.VMEM((shards * 8, 128), f32),
+            pltpu.VMEM((own_key.shape[1] // HD, kv_rows, 128), bf16),
+            pltpu.VMEM((shards, kv_rows, 128), bf16),
+            pltpu.VMEM((shards * 16, 128), f32),
+            pltpu.VMEM((shards * local_rows, 128), f32),
+            pltpu.VMEM((shards * size, 128), f32),
+            pltpu.VMEM((size, 128), f32),
+            pltpu.VMEM((size, 128), bf16),
+            pltpu.VMEM((shards, size, 128), bf16),
+            pltpu.VMEM((shards * size, 128), f32),
+            pltpu.VMEM((shards * local_rows, width), bf16),
+        ]
+        + boxes
+        + boxes
+        + [pltpu.SemaphoreType.DMA((shards,))] * 10,
+        compiler_params=pltpu.CompilerParams(collective_id=1, has_side_effects=True),
+        name="fused_layer",
+    )(
+        prefix_of_row,
+        context_len,
+        gate_up_scales,
+        down_scales,
+        queries,
+        own_key,
+        own_value,
+        cache_keys,
+        cache_values,
+        hidden_in,
+        norm_gain.reshape(lanes, 128),
+        expert_ids,
+        route_weights,
+        w_out,
+        gate_up_codes,
+        down_codes,
+    )
+
+
+def fits_fused(queries, own_key, cache_keys, w_out, expert_ids):
+    shards = lax.axis_size("ctx")
+    local_rows, width = queries.shape
+    return (
+        shards % 8 == 0
+        and shards & (shards - 1) == 0
+        and w_out.shape[0] == HD
+        and width == shards * HD
+        and w_out.shape[1] == width
+        and 2 * local_rows == 8
+        and shards % (own_key.shape[1] // HD * 8) == 0
+        and shards * local_rows % CAND == 0
+        and cache_keys.shape[1] % 16 == 0
+    )
+
+
+def local(*arrays):
+    queries, own_key, cache_keys = arrays[0], arrays[1], arrays[3]
+    if fits_fused(queries, own_key, cache_keys, arrays[8], arrays[10]):
+        return fused_layer(*arrays)
+    return staged_layer(*arrays)
+
+
 def solution(mesh):
     return jax.shard_map(
         local,

time: 167 us -> 66.5 us (0.40)
  waiting for transfers between devices: 32.8 us -> 0 us
  starting transfers between devices: 24.5 us -> 0 us
  local copies, waits for them, and re-layouts: 25.8 us -> 5.4 us
  matrix products: 12 us -> 0 us
  other arithmetic: 11.9 us -> 0 us
  Pallas kernels: 56.8 us -> 60.1 us
  between operations: 2.56 us -> 0.64 us
    ppermute x17 -> x0, waiting for transfers between devices: 25.8 us -> none  [swapped(): lax.ppermute(value, axis, [(i, i ^ 1 << distance) for i in range(lax.axis...]
    ppermute x17 -> x0, starting transfers between devices: 20.4 us -> none  [swapped(): lax.ppermute(value, axis, [(i, i ^ 1 << distance) for i in range(lax.axis...]
    dot_general x6 -> x0, matrix products: 12 us -> none  [the longest x1 4.99 us: local(): jnp.dot(flat_rows, gate_up, preferred_element_type=jnp.float32)]
    convert_element_type x4 -> x0, other arithmetic: 8.25 us -> none  [the longest x1 7.36 us: dequantize(): return (code_values.astype(jnp.float32) * spread).astype(jnp.bfloat16)]
    all_to_all x1 -> x0, waiting for transfers between devices: 7.06 us -> none  [local(): lax.all_to_all(attended, 'ctx', split_axis=1, concat_axis=0, tiled=True)]
    reshape x10 -> x0, local copies, waits for them, and re-layouts: 6.57 us -> none  [the longest x1 1.32 us: local(): result.reshape(shards, local_rows * lanes, 128)]
    unnamed x28 -> x4, local copies, waits for them, and re-layouts: 9.92 us -> 5.4 us
    all_to_all x1 -> x0, starting transfers between devices: 4.01 us -> none  [local(): lax.all_to_all(attended, 'ctx', split_axis=1, concat_axis=0, tiled=True)]
  transfers between devices with their start and end apart: 18 -> 0, of which waited for: 10 -> 0; matrix products, arithmetic and copies ran while one was open for 14% -> 0% of each run, Pallas kernels for 0% -> 0%
where the time goes in v1:
time: 66.5 us; the launch traced here: 66.1 us
  Pallas kernels  60.1 us (90%)
  local copies, waits for them, and re-layouts  5.4 us (8%)
    pallas_call x1, Pallas kernels, fused_layer(): pl.pallas_call(lambda *refs: layer_kernel(shards, CAND // local_rows, *re...  60.1 us
    unnamed x4, local copies, waits for them, and re-layouts  5.4 us

profile of v1, /device:TPU:0, one launch (start us, length us, event | category | flops | bytes accessed | tf_op | source)
XLA Modules:
  0.0 66.1 jit_solution(5749710819532962307)
XLA Ops:
  0.6 1.3 %copy.19.refs_3_ = f32[1,3,32]{2,1,0:T(4,128)} copy(f32[1,3,32]{2,0,1:T(1,128)} %param.31) | data formatting | bytes 768 | tf_op args[15]
  1.9 1.4 %copy.18.refs_2_ = f32[1,32,6]{2,1,0:T(8,128)} copy(f32[1,32,6]{1,0,2:T(1,128)} %param.29) | data formatting | bytes 1536 | tf_op args[13]
  3.3 60.1 %fused_layer.1 = (bf16[4,4096]{1,0:T(4,128)(2,1)}, bf16[4,4096]{1,0:T(4,128)(2,1)}) custom-call(s32[128]{0:T(128)} %refs_0_.1, s32[2]{0:T(128)} %refs_1_.1, f32[1,32,6]{2,1,0:T(8,128)} %copy.18.refs_2_, f32[1,3,32]{2,1,0:T(4,128)} %copy.19.refs_3_, bf16[4,4096]{1,0:T(4,128)(2,1)} %refs_4_.1, bf16[4,256]{1,0:T(4,128)(2,1)} %refs_5_.1, ...), custom_call_target="tpu_custom_call" | custom-call | tf_op jit(solution)/shard_map/fused_layer/pallas_call | solution.py:857
  63.4 1.4 %copy.22 = bf16[4,4096]{1,0:T(4,128)(2,1)} copy(bf16[4,4096]{1,0:T(4,128)(2,1)} %get-tuple-element.4) | data formatting | bytes 65536
  64.8 1.4 %copy.23 = bf16[4,4096]{1,0:T(4,128)(2,1)} copy(bf16[4,4096]{1,0:T(4,128)(2,1)} %get-tuple-element.5) | data formatting | bytes 65536

commit v2 on v1

--- a/solution.py
+++ b/solution.py
@@ -13,6 +13,7 @@
 
 NEG = -1e30
 EPSILON = 1e-06
+VMEM_BYTES = None
 
 
 def swapped(value, axis, distance):
@@ -523,46 +524,47 @@
 def layer_kernel(
     shards,
     per_block,
-    prefix_ref,
-    length_ref,
-    gate_scale_ref,
-    down_scale_ref,
-    queries_ref,
-    own_key_ref,
-    own_value_ref,
-    keys_ref,
-    values_ref,
-    hidden_ref,
-    gain_ref,
-    ids_ref,
-    route_ref,
-    w_out_hbm,
-    gate_hbm,
-    down_hbm,
-    attention_ref,
-    layer_ref,
-    w_out_ref,
-    gate_ref,
-    down_ref,
-    load_sem,
-    stage,
-    q_send,
-    q_column,
-    q_plane,
-    q_all,
-    q_wide,
-    kv_send,
-    kv_all,
-    own_wide,
-    attended,
-    partial,
-    mixed_ref,
-    normed_send,
-    normed_all,
-    rows_wide,
-    rows_ref,
-    *boxes_and_sems,
+    *refs,
 ):
+    given, (mixed_out, expert_out), refs = refs[:16], refs[16:18], refs[18:]
+    held, load_sem = refs[:16], refs[16]
+    (
+        prefix_ref,
+        length_ref,
+        keys_ref,
+        values_ref,
+        own_key_ref,
+        own_value_ref,
+        queries_ref,
+        ids_ref,
+        route_ref,
+        w_out_ref,
+        gate_ref,
+        gate_scale_ref,
+        down_ref,
+        down_scale_ref,
+        hidden_ref,
+        gain_ref,
+    ) = held
+    (
+        stage,
+        q_send,
+        q_column,
+        q_plane,
+        q_all,
+        q_wide,
+        kv_send,
+        kv_all,
+        own_wide,
+        attended,
+        partial,
+        mixed_ref,
+        normed_send,
+        normed_all,
+        rows_wide,
+        rows_ref,
+    ) = refs[17 : 17 + 16]
+    boxes_and_sems = refs[17 + 16 :]
     first_boxes, second_boxes = boxes_and_sems[0:6], boxes_and_sems[6:12]
     sems = boxes_and_sems[12:]
     q_sems, kv_sems, first_sems, row_sems, second_sems = [sems[2 * i : 2 * i + 2] for i in range(5)]
@@ -579,14 +581,14 @@
     score_scale = 1.0 / math.sqrt(HD)
     f32 = jnp.float32
 
+    place.greet()
     loads = []
-    for i, (source, target) in enumerate(
-        ((w_out_hbm, w_out_ref), (gate_hbm.at[0], gate_ref), (down_hbm.at[0], down_ref))
-    ):
+    for i, (source, target) in enumerate(zip(given, held)):
         load = pltpu.make_async_copy(source, target, load_sem.at[i])
         load.start()
         loads.append(load)
-    place.greet()
+    for load in loads[:9]:
+        load.wait()
 
     lengths = []
     for b in range(blocks):
@@ -667,26 +669,28 @@
     my_group = me // per_group
 
     def dequantize_gate():
-        loads[1].wait()
+        loads[10].wait()
+        loads[11].wait()
 
         def block_row(i, carry):
             at = pl.ds(pl.multiple_of(i * 128, 128), 128)
             for j in range(gate_ref.shape[1] // 128):
                 cut = slice(j * 128, (j + 1) * 128)
-                wide = gate_ref[at, cut].astype(f32) * gate_scale_ref[0, i, j]
+                wide = gate_ref[at, cut].astype(f32) * gate_scale_ref[j, 0, i]
                 gate_ref[at, cut] = wide.astype(jnp.bfloat16)
             return carry
 
         lax.fori_loop(0, gate_ref.shape[0] // 128, block_row, 0)
 
     def dequantize_down():
-        loads[2].wait()
+        loads[12].wait()
+        loads[13].wait()
 
         def block_column(j, carry):
             at = pl.ds(pl.multiple_of(j * 128, 128), 128)
             for i in range(down_ref.shape[0] // 128):
                 cut = slice(i * 128, (i + 1) * 128)
-                wide = down_ref[cut, at].astype(f32) * down_scale_ref[0, i, j]
+                wide = down_ref[cut, at].astype(f32) * down_scale_ref[i, 0, j]
                 down_ref[cut, at] = wide.astype(jnp.bfloat16)
             return carry
 
@@ -747,7 +751,7 @@
                     r * shards : (r + 1) * shards, i * 128 : (i + 1) * 128
                 ]
 
-    loads[0].wait()
+    loads[9].wait()
     head_rows = attended[...].astype(jnp.bfloat16)
     for i in range(0, width, 512):
         scatter_rows(
@@ -757,6 +761,8 @@
     projected, more = collect(place, partial, size, first_boxes, first_sems, dequantize_down)
     waits = waits + more
 
+    loads[14].wait()
+    loads[15].wait()
     for i in range(lanes):
         mixed_ref[pl.ds(i, local_rows, stride=lanes), :] = hidden_ref[
             :, i * 128 : (i + 1) * 128
@@ -777,9 +783,9 @@
 
     def write_attention():
         for i in range(lanes):
-            attention_ref[:, i * 128 : (i + 1) * 128] = mixed_ref[
+            mixed_out[:, i * 128 : (i + 1) * 128] = mixed_ref[
                 pl.ds(i, local_rows, stride=lanes), :
-            ].astype(jnp.bfloat16)
+            ]
 
     more = spread(
         place,
@@ -811,11 +817,9 @@
         )
     expert_sum, more = collect(place, partial, size, second_boxes, second_sems, lambda: None)
     waits = waits + more
-    mixed_ref[...] = mixed_ref[...] + expert_sum
+    mixed_ref[...] = expert_sum
     for i in range(lanes):
-        layer_ref[:, i * 128 : (i + 1) * 128] = mixed_ref[
-            pl.ds(i, local_rows, stride=lanes), :
-        ].astype(jnp.bfloat16)
+        expert_out[:, i * 128 : (i + 1) * 128] = mixed_ref[pl.ds(i, local_rows, stride=lanes), :]
     for copy in waits + list(q_copies.values()):
         copy.wait_send()
 
@@ -850,20 +854,38 @@
         pltpu.VMEM((count, size, 128), bf16)
         for count in (shards // 2, shards // 2, shards // 2, shards // 2, column, column)
     ]
-    smem = pl.BlockSpec(memory_space=pltpu.SMEM)
+    operands = (
+        prefix_of_row,
+        context_len,
+        cache_keys,
+        cache_values,
+        own_key,
+        own_value,
+        queries,
+        expert_ids,
+        route_weights,
+        w_out,
+        gate_up_codes[0],
+        gate_up_scales.transpose(2, 0, 1),
+        down_codes[0],
+        down_scales.transpose(1, 0, 2),
+        hidden_in,
+        norm_gain.reshape(lanes, 128),
+    )
+    scalars = (0, 1, 11, 13)
+    out = jax.ShapeDtypeStruct((local_rows, width), f32)
     vmem = pl.BlockSpec(memory_space=pltpu.VMEM)
-    hbm = pl.BlockSpec(memory_space=pl.ANY)
-    out = jax.ShapeDtypeStruct((local_rows, width), bf16)
-    return pl.pallas_call(
+    mixed, expert_sum = pl.pallas_call(
         lambda *refs: layer_kernel(shards, CAND // local_rows, *refs),
         out_shape=(out, out),
-        in_specs=[smem] * 4 + [vmem] * 9 + [hbm] * 3,
+        in_specs=[pl.BlockSpec(memory_space=pltpu.HBM)] * len(operands),
         out_specs=(vmem, vmem),
         scratch_shapes=[
-            pltpu.VMEM(w_out.shape, bf16),
-            pltpu.VMEM(gate_up_codes.shape[1:], bf16),
-            pltpu.VMEM(down_codes.shape[1:], bf16),
-            pltpu.SemaphoreType.DMA((3,)),
+            (pltpu.SMEM if i in scalars else pltpu.VMEM)(x.shape, x.dtype)
+            for i, x in enumerate(operands)
+        ]
+        + [
+            pltpu.SemaphoreType.DMA((len(operands),)),
             pltpu.VMEM((shards * 8, 128), f32),
             pltpu.VMEM((shards, 8, 128), bf16),
             pltpu.VMEM((column, 8, 8, 128), bf16),
@@ -884,26 +906,12 @@
         + boxes
         + boxes
         + [pltpu.SemaphoreType.DMA((shards,))] * 10,
-        compiler_params=pltpu.CompilerParams(collective_id=1, has_side_effects=True),
+        compiler_params=pltpu.CompilerParams(
+            collective_id=1, has_side_effects=True, vmem_limit_bytes=VMEM_BYTES
+        ),
         name="fused_layer",
-    )(
-        prefix_of_row,
-        context_len,
-        gate_up_scales,
-        down_scales,
-        queries,
-        own_key,
-        own_value,
-        cache_keys,
-        cache_values,
-        hidden_in,
-        norm_gain.reshape(lanes, 128),
-        expert_ids,
-        route_weights,
-        w_out,
-        gate_up_codes,
-        down_codes,
-    )
+    )(*operands)
+    return mixed.astype(bf16), (mixed + expert_sum).astype(bf16)
 
 
 def fits_fused(queries, own_key, cache_keys, w_out, expert_ids):

time: 66.5 us -> 61.5 us (0.925)
  local copies, waits for them, and re-layouts: 5.4 us -> 0 us
  other arithmetic: 0 us -> 1.57 us
  Pallas kernels: 60.1 us -> 59.1 us
    unnamed x4 -> x0, local copies, waits for them, and re-layouts: 5.4 us -> none
    convert_element_type x0 -> x1, other arithmetic: none -> 1.57 us  [fused_layer(): return (mixed.astype(bf16), (mixed + expert_sum).astype(bf16))]
    pallas_call x1, Pallas kernels: 60.1 us -> 59.1 us  [fused_layer(): pl.pallas_call(lambda *refs: layer_kernel(shards, CAND // local_rows, *re...]
where the time goes in v2:
time: 61.5 us; the launch traced here: 61.4 us
  Pallas kernels  59.1 us (96%)
  other arithmetic  1.57 us (3%)
  between operations  0.64 us (1%)
    pallas_call x1, Pallas kernels, fused_layer(): pl.pallas_call(lambda *refs: layer_kernel(shards, CAND // local_rows, *re...  59.1 us
    convert_element_type x1, other arithmetic, fused_layer(): return (mixed.astype(bf16), (mixed + expert_sum).astype(bf16))  1.57 us

profile of v2, /device:TPU:0, one launch (start us, length us, event | category | flops | bytes accessed | tf_op | source)
XLA Modules:
  0.0 61.4 jit_solution(13088638068105401602)
XLA Ops:
  0.6 59.1 %fused_layer.1 = (f32[4,4096]{1,0:T(4,128)}, f32[4,4096]{1,0:T(4,128)}) custom-call(s32[128]{0:T(128)} %refs_0_.1, s32[2]{0:T(128)} %refs_1_.1, bf16[2,32,256]{2,1,0:T(8,128)(2,1)} %refs_2_.1, bf16[2,32,256]{2,1,0:T(8,128)(2,1)} %refs_3_.1, bf16[4,256]{1,0:T(4,128)(2,1)} %refs_4_.1, bf16[4,256]{1,0:T(4,128)(2,1)} %refs_5_.1, bf16[4,4096]{1,0:T(4,128)(2,1)} %refs_6_.1, ...), custom_call_target="tpu_custom_call" | custom-call | tf_op jit(solution)/shard_map/fused_layer/pallas_call | solution.py:878
  59.8 1.6 %add_convert_fusion = (bf16[4,4096]{1,0:T(4,128)(2,1)}, bf16[4,4096]{1,0:T(4,128)(2,1)}) fusion(f32[4,4096]{1,0:T(4,128)} %get-tuple-element.4, f32[4,4096]{1,0:T(4,128)} %get-tuple-element.5), kind=kLoop, calls=%fused_computation | loop fusion | flops 49152 | bytes 196608 | tf_op jit(solution)/shard_map/convert_element_type | solution.py:914

commit v3 on v2

--- a/solution.py
+++ b/solution.py
@@ -421,104 +421,133 @@
         pl.semaphore_wait(pltpu.get_barrier_semaphore(), len(self.peers()))
 
 
-def spread(place, column_source, own, buffer, sems, on_column, on_plane, on_core, filler):
+def arrived(ref, sem):
+    pltpu.make_async_copy(ref, ref, sem).wait()
+
+
+def spread(place, column_source, buffer, sems, on_start, on_column, on_plane, on_core, filler):
     send_sem, recv_sem = sems
-    copies = {}
-
-    def post(source, block, slot, towards):
-        copies[slot] = remote(
-            source,
-            buffer.at[place.peer(block)],
-            send_sem.at[slot],
-            recv_sem.at[slot],
-            place.peer(towards),
+    column = place.column
+
+    def post(kind, source, target, slot, towards):
+        return remote(
+            source, target, send_sem.at[kind], recv_sem.at[slot], place.peer(towards)
         )
 
     def forward(k):
-        source = own if k == 0 else buffer.at[place.peer(k * 8)]
-        for plane in (6, 2, 4):
-            post(source, k * 8, k * 8 + plane, plane)
-        post(source, k * 8, k * 8 + 1, 1)
-
-    for k in reversed(range(1, place.column)):
-        post(column_source(k), 0, k * 8, k * 8)
+        for plane in (3, 1, 2):
+            post(1, buffer.at[k, 0, 0], buffer.at[k, plane, 0], column + k, plane * 2)
+
+    for k in reversed(range(1, column)):
+        post(0, column_source(k), buffer.at[k, 0, 0], k, k * 8)
     forward(0)
+    on_start()
     on_column(0)
-    for k in range(1, place.column):
-        copies[k * 8].wait_recv()
+    for k in range(1, column):
+        arrived(buffer.at[k, 0, 0], recv_sem.at[k])
         forward(k)
         on_column(k)
     filler()
-    for k in range(place.column):
-        on_plane(k * 8)
-        for plane in (2, 4, 6):
-            slot = k * 8 + plane
-            copies[slot].wait_recv()
-            post(buffer.at[place.peer(slot)], slot, slot + 1, 1)
-            on_plane(slot)
-    for slot in range(0, place.shards, 2):
-        copies[slot + 1].wait_recv()
-        on_core(slot + 1)
-    return list(copies.values())
-
-
-def collect(place, values, size, boxes, sems, filler):
-    send_sem, recv_sem = sems
-    core_out, core_in, plane_out, plane_in, column_out, column_in = boxes
-    kind = core_out.dtype
-    copies = {}
-    chips = place.shards // 2
-
-    def held(pattern):
-        start = pl.multiple_of(place.peer(pattern) * size, size)
-        return values[pl.ds(start, size), :]
-
-    order = [k * 4 + p for k in reversed(range(place.column)) for p in (3, 1, 2)]
-    order = order + [k * 4 for k in reversed(range(place.column))]
-    for chip in order:
-        core_out[chip] = held(chip * 2 + 1).astype(kind)
-        copies[chip] = remote(
-            core_out.at[chip], core_in.at[chip], send_sem.at[chip], recv_sem.at[chip], place.peer(1)
+    for k in range(column):
+        arrived(buffer.at[k, pl.ds(1, 3), 0], recv_sem.at[column + k])
+        post(2, buffer.at[k, :, 0], buffer.at[k, :, 1], 2 * column + k, 1)
+        on_plane(k)
+    for k in range(column):
+        arrived(buffer.at[k, :, 1], recv_sem.at[2 * column + k])
+        on_core(k)
+    return [
+        (buffer.at[pl.ds(1, column - 1), 0, 0], send_sem.at[0]),
+        (buffer.at[:, pl.ds(1, 3), 0], send_sem.at[1]),
+        (buffer.at[:, :, 0], send_sem.at[2]),
+    ]
+
+
+class Collect:
+    def __init__(self, place, values, size, boxes, sems):
+        self.place, self.values, self.size = place, values, size
+        self.half = size // 2
+        self.core_out, self.core_in, self.plane_out, self.plane_in = boxes[0:4]
+        self.column_out, self.column_in = boxes[4:6]
+        self.kind = self.core_out.dtype
+        self.send_sem, self.recv_sem = sems
+
+    def post(self, kind, slot, out_box, in_box, at, towards):
+        remote(
+            out_box.at[at],
+            in_box.at[at],
+            self.send_sem.at[kind],
+            self.recv_sem.at[slot],
+            self.place.peer(towards),
         )
 
-    def on_chip(chip):
-        copies[chip].wait_recv()
-        return held(chip * 2) + core_in[chip].astype(jnp.float32)
-
-    for k in reversed(range(place.column)):
-        for p in (3, 1, 2):
-            chip = k * 4 + p
-            plane_out[chip] = on_chip(chip).astype(kind)
-            copies[chips + chip] = remote(
-                plane_out.at[chip],
-                plane_in.at[chip],
-                send_sem.at[chips + chip],
-                recv_sem.at[chips + chip],
-                place.peer(p * 2),
+    def slot(self, kind, half, k):
+        return (kind * 2 + half) * self.place.column + k
+
+    def held(self, half, pattern):
+        start = self.place.peer(pattern) * self.size + half * self.half
+        return self.values[pl.ds(pl.multiple_of(start, self.half), self.half), :]
+
+    def core(self, half):
+        for k in reversed(range(self.place.column)):
+            for plane in range(4):
+                self.core_out[half, k, plane] = self.held(half, k * 8 + plane * 2 + 1).astype(
+                    self.kind
+                )
+            self.post(0, self.slot(0, half, k), self.core_out, self.core_in, (half, k), 1)
+
+    def chip(self, half, k, plane):
+        return self.held(half, k * 8 + plane * 2) + self.core_in[half, k, plane].astype(jnp.float32)
+
+    def plane(self, half, k):
+        arrived(self.core_in.at[half, k], self.recv_sem.at[self.slot(0, half, k)])
+        for plane in (3, 1, 2):
+            at = (half, k, plane)
+            self.plane_out[at] = self.chip(half, k, plane).astype(self.kind)
+            self.post(
+                1, self.slot(1, half, k), self.plane_out, self.plane_in, at, plane * 2
             )
-    filler()
-
-    def on_plane(k):
-        total = on_chip(k * 4)
-        for p in (1, 2, 3):
-            copies[chips + k * 4 + p].wait_recv()
-            total = total + plane_in[k * 4 + p].astype(jnp.float32)
+
+    def own(self, half, k):
+        total = self.chip(half, k, 0)
+        arrived(
+            self.plane_in.at[half, k, pl.ds(1, 3)], self.recv_sem.at[self.slot(1, half, k)]
+        )
+        for plane in (1, 2, 3):
+            total = total + self.plane_in[half, k, plane].astype(jnp.float32)
         return total
 
-    for k in reversed(range(1, place.column)):
-        column_out[k] = on_plane(k).astype(kind)
-        copies[chips + k * 4] = remote(
-            column_out.at[k],
-            column_in.at[k],
-            send_sem.at[chips + k * 4],
-            recv_sem.at[chips + k * 4],
-            place.peer(k * 8),
+    def column(self, half, k):
+        at = (half, k)
+        self.column_out[at] = self.own(half, k).astype(self.kind)
+        self.post(
+            2, 4 * self.place.column + half, self.column_out, self.column_in, at, k * 8
         )
-    total = on_plane(0)
-    for k in range(1, place.column):
-        copies[chips + k * 4].wait_recv()
-        total = total + column_in[k].astype(jnp.float32)
-    return total, list(copies.values())
+
+    def run(self, fill, filler):
+        steps = [(half, k) for k in reversed(range(1, self.place.column)) for half in range(2)]
+        fill(0)
+        self.core(0)
+        fill(1)
+        self.plane(*steps[0])
+        self.core(1)
+        for step in steps[1:] + [(0, 0), (1, 0)]:
+            self.plane(*step)
+        filler()
+        for step in steps:
+            self.column(*step)
+        totals = [self.own(half, 0) for half in range(2)]
+        others = pl.ds(1, self.place.column - 1)
+        for half in range(2):
+            arrived(
+                self.column_in.at[half, others], self.recv_sem.at[4 * self.place.column + half]
+            )
+            for k in range(1, self.place.column):
+                totals[half] = totals[half] + self.column_in[half, k].astype(jnp.float32)
+        return jnp.concatenate(totals, axis=0), [
+            (self.core_out, self.send_sem.at[0]),
+            (self.plane_out.at[:, :, pl.ds(1, 3)], self.send_sem.at[1]),
+            (self.column_out.at[:, others], self.send_sem.at[2]),
+        ]
 
 
 def layer_kernel(
@@ -551,7 +580,7 @@
         q_send,
         q_column,
         q_plane,
-        q_all,
+        q_core,
         q_wide,
         kv_send,
         kv_all,
@@ -559,12 +588,11 @@
         attended,
         partial,
         mixed_ref,
-        normed_send,
         normed_all,
         rows_wide,
         rows_ref,
-    ) = refs[17 : 17 + 16]
-    boxes_and_sems = refs[17 + 16 :]
+    ) = refs[17 : 17 + 15]
+    boxes_and_sems = refs[17 + 15 :]
     first_boxes, second_boxes = boxes_and_sems[0:6], boxes_and_sems[6:12]
     sems = boxes_and_sems[12:]
     q_sems, kv_sems, first_sems, row_sems, second_sems = [sems[2 * i : 2 * i + 2] for i in range(5)]
@@ -580,6 +608,11 @@
     per_group = shards // key_groups
     score_scale = 1.0 / math.sqrt(HD)
     f32 = jnp.float32
+    half_lanes = lanes // 2
+
+    def lane_at(i):
+        return i // half_lanes * (size // 2) + i % half_lanes
+
 
     place.greet()
     loads = []
@@ -607,64 +640,49 @@
                 kv_send[g, at : at + positions, :] = chosen[:, g * HD : (g + 1) * HD].astype(
                     jnp.bfloat16
                 )
+    stage[...] = jnp.zeros((16, HD), f32)
+    lane = lax.broadcasted_iota(jnp.int32, (local_rows, 128), 1)
+    dense = jnp.zeros((local_rows, 128), f32)
+    for choice in range(ids_ref.shape[1]):
+        dense = dense + jnp.where(
+            lane % 64 == ids_ref[:, choice : choice + 1], route_ref[:, choice : choice + 1], 0.0
+        )
+    coarse = dense.astype(jnp.bfloat16).astype(f32)
+    stage[local_rows : 2 * local_rows, :] = jnp.where(lane < 64, coarse, dense - coarse)
     for g in range(key_groups):
         cut = slice(g * HD, (g + 1) * HD)
-        stage[0:16, :] = jnp.zeros((16, HD), f32)
         stage[0:local_rows, :] = own_key_ref[:, cut].astype(f32)
         stage[8 : 8 + local_rows, :] = own_value_ref[:, cut].astype(f32)
-        kv_send[g, 2 * span : 2 * span + 16, :] = stage[0:16, :].astype(jnp.bfloat16)
-    lane = lax.broadcasted_iota(jnp.int32, (local_rows, 128), 1)
-    for expert in range(shards // 2):
-        weight = jnp.sum(
-            jnp.where(ids_ref[...] == expert, route_ref[...], 0.0), axis=1, keepdims=True
-        )
-        weight = jnp.broadcast_to(weight, (local_rows, 128))
-        coarse = weight.astype(jnp.bfloat16).astype(f32)
-        both = jnp.where(lane < 64, coarse, weight - coarse)
-        for d in (2 * expert, 2 * expert + 1):
-            stage[8 * d : 8 * d + local_rows, :] = queries_ref[:, d * HD : (d + 1) * HD].astype(f32)
-            stage[8 * d + local_rows : 8 * d + 2 * local_rows, :] = both
-    q_send[...] = stage[...].reshape(shards, 8, 128).astype(jnp.bfloat16)
+        kv_send[g, 2 * span : 2 * span + 16, :] = stage[...].astype(jnp.bfloat16)
+    for d in range(shards):
+        q_send[d] = queries_ref[:, d * HD : (d + 1) * HD]
     place.met()
 
-    q_copies = {}
-
-    def q_post(source, target, slot, towards):
-        q_copies[slot] = remote(
-            source, target, q_sems[0].at[slot], q_sems[1].at[slot], place.peer(towards)
-        )
-
-    def q_blocks(slot, start, count):
-        k, plane = slot // 8, slot % 8 // 2
-        if plane:
-            return q_plane.at[k * 4 + plane, pl.ds(start % 2, count)]
-        if k:
-            return q_column.at[k, pl.ds(start % 8, count)]
-        return q_send.at[pl.ds(start, count)]
-
-    for k in reversed(range(1, place.column)):
-        q_post(q_send.at[pl.ds(place.peer(k * 8) // 8 * 8, 8)], q_column.at[k], k * 8, k * 8)
+    column = place.column
+
+    def q_post(kind, source, target, slot, towards):
+        remote(source, target, q_sems[0].at[kind], q_sems[1].at[slot], place.peer(towards))
+
+    def q_start():
+        for k in reversed(range(1, column)):
+            first = place.peer(k * 8) // 8 * 8
+            q_post(0, q_send.at[pl.ds(first, 8)], q_column.at[k], k, k * 8)
+        q_column[0] = q_send[pl.ds(me // 8 * 8, 8)]
 
     def q_on_column(k):
         if k:
-            q_copies[k * 8].wait_recv()
+            arrived(q_column.at[k], q_sems[1].at[k])
         for plane in (3, 1, 2):
-            start = place.peer(plane * 2) // 2 * 2
-            q_post(
-                q_blocks(k * 8, start, 2), q_plane.at[k * 4 + plane], k * 8 + plane * 2, plane * 2
-            )
-
-    def q_on_plane(slot):
-        if slot % 8:
-            q_copies[slot].wait_recv()
-        origin = place.peer(slot)
-        q_post(
-            q_blocks(slot, place.peer(1), 1), q_all.at[pl.ds(origin, 1)], slot + 1, 1
-        )
-        q_all[pl.ds(origin, 1)] = q_blocks(slot, me, 1)[...]
-
-    def q_on_core(slot):
-        q_copies[slot].wait_recv()
+            first = place.peer(plane * 2) % 8 // 2 * 2
+            source = (q_column.at[k] if k else q_send).at[
+                pl.ds(first + (0 if k else me // 8 * 8), 2)
+            ]
+            q_post(1, source, q_plane.at[k, plane], column + k, plane * 2)
+        q_plane[k, 0] = q_column[k, pl.ds(me % 8 // 2 * 2, 2)]
+
+    def q_on_plane(k):
+        arrived(q_plane.at[k, pl.ds(1, 3)], q_sems[1].at[column + k])
+        q_post(2, q_plane.at[k, :, place.peer(1) % 2], q_core.at[k], 2 * column, 1)
 
     my_group = me // per_group
 
@@ -696,23 +714,36 @@
 
         lax.fori_loop(0, down_ref.shape[1] // 128, block_column, 0)
 
-    kv_all[pl.ds(me, 1)] = kv_send[pl.ds(my_group, 1)]
+    kv_all[0, 0, 0] = kv_send[my_group]
     waits = spread(
         place,
         lambda k: kv_send.at[place.peer(k * 8) // per_group],
-        kv_send.at[my_group],
         kv_all,
         kv_sems,
+        q_start,
         q_on_column,
         q_on_plane,
-        q_on_core,
+        lambda k: None,
         dequantize_gate,
     )
 
-    q_wide[...] = q_all[...].astype(f32).reshape(shards * 8, 128)
-    own_wide[...] = kv_all[:, 2 * span : 2 * span + 16, :].astype(f32).reshape(shards * 16, 128)
+    waits = waits + [
+        (q_column.at[pl.ds(1, column - 1)], q_sems[0].at[0]),
+        (q_plane.at[:, pl.ds(1, 3)], q_sems[0].at[1]),
+        (q_core, q_sems[0].at[2]),
+    ]
+    arrived(q_core, q_sems[1].at[2 * column])
+    for k in range(column):
+        for plane in range(4):
+            for core, block in ((0, q_plane[k, plane, me % 2]), (1, q_core[k, plane])):
+                device = place.peer(k * 8 + plane * 2 + core)
+                q_wide[pl.ds(pl.multiple_of(device * 8, 8), local_rows), :] = block.astype(f32)
+                own_wide[pl.ds(pl.multiple_of(device * 16, 16), 16), :] = kv_all[
+                    k, plane, core, 2 * span : 2 * span + 16
+                ].astype(f32)
     total_positions = shards * positions
-    position = lax.broadcasted_iota(jnp.int32, (1, total_positions), 1)
+    counted = lax.broadcasted_iota(jnp.int32, (1, total_positions), 1)
+    position = (counted // positions ^ me) * positions + counted % positions
 
     def picked(ref, start, count, stride):
         return jnp.concatenate(
@@ -722,8 +753,8 @@
     for b in range(blocks):
         first = b * per_block
         key_at, value_at = b * positions, span + b * positions
-        key = kv_all[:, key_at : key_at + positions, :].reshape(total_positions, HD)
-        value = kv_all[:, value_at : value_at + positions, :].reshape(total_positions, HD)
+        key = kv_all[:, :, :, key_at : key_at + positions, :].reshape(total_positions, HD)
+        value = kv_all[:, :, :, value_at : value_at + positions, :].reshape(total_positions, HD)
         query = picked(q_wide, first * 8, per_block, 8)
         own_k = picked(own_wide, first * 16, per_block, 16)
         own_v = picked(own_wide, first * 16 + 8, per_block, 16)
@@ -744,84 +775,88 @@
                 r * per_block : (r + 1) * per_block, :
             ]
 
-    def scatter_rows(result, first_lane):
-        for i in range(result.shape[1] // 128):
-            for r in range(local_rows):
-                partial[pl.ds(r * lanes + first_lane + i, shards, stride=size), :] = result[
-                    r * shards : (r + 1) * shards, i * 128 : (i + 1) * 128
-                ]
+    def multiply_out(rows, matrix_ref, half):
+        for first in range(half * width // 2, (half + 1) * width // 2, 512):
+            result = jnp.dot(
+                rows, matrix_ref[:, first : first + 512], preferred_element_type=f32
+            )
+            for i in range(4):
+                for r in range(local_rows):
+                    start = lane_at(first // 128 + i) + r * half_lanes
+                    partial[pl.ds(start, shards, stride=size), :] = result[
+                        r * shards : (r + 1) * shards, i * 128 : (i + 1) * 128
+                    ]
 
     loads[9].wait()
     head_rows = attended[...].astype(jnp.bfloat16)
-    for i in range(0, width, 512):
-        scatter_rows(
-            jnp.dot(head_rows, w_out_ref[:, i : i + 512], preferred_element_type=f32), i // 128
-        )
-
-    projected, more = collect(place, partial, size, first_boxes, first_sems, dequantize_down)
+    total = Collect(place, partial, size, first_boxes, first_sems)
+    projected, more = total.run(
+        lambda half: multiply_out(head_rows, w_out_ref, half), dequantize_down
+    )
     waits = waits + more
 
     loads[14].wait()
     loads[15].wait()
     for i in range(lanes):
-        mixed_ref[pl.ds(i, local_rows, stride=lanes), :] = hidden_ref[
+        mixed_ref[pl.ds(lane_at(i), local_rows, stride=half_lanes), :] = hidden_ref[
             :, i * 128 : (i + 1) * 128
         ].astype(f32)
     mixed = mixed_ref[...] + projected
     mixed_ref[...] = mixed
-    grouped = mixed.reshape(local_rows, lanes, 128)
-    mean_square = (
-        jnp.sum(jnp.sum(grouped * grouped, axis=1, keepdims=True), axis=2, keepdims=True) / width
-    )
-    normed = grouped * lax.rsqrt(mean_square + EPSILON) * gain_ref[...][None]
-    normed_send[...] = normed.reshape(size, 128).astype(jnp.bfloat16)
-
-    def widen(slot):
-        at = pl.ds(pl.multiple_of(place.peer(slot) * size, size), size)
-        block = normed_all[place.peer(slot)] if slot else normed_send[...]
-        rows_wide[at, :] = block.astype(f32)
+    grouped = mixed.reshape(2, local_rows, half_lanes, 128)
+    squares = jnp.sum(grouped * grouped, axis=2, keepdims=True)
+    squares = jnp.sum(jnp.sum(squares, axis=0, keepdims=True), axis=3, keepdims=True)
+    gain = gain_ref[...].reshape(2, 1, half_lanes, 128)
+    normed = grouped * lax.rsqrt(squares / width + EPSILON) * gain
+    normed_all[0, 0, 0] = normed.reshape(size, 128).astype(jnp.bfloat16)
+
+    def widen(k, core):
+        for plane in range(4):
+            device = place.peer(k * 8 + plane * 2 + core)
+            at = pl.ds(pl.multiple_of(device * size, size), size)
+            rows_wide[at, :] = normed_all[k, plane, core].astype(f32)
 
     def write_attention():
         for i in range(lanes):
             mixed_out[:, i * 128 : (i + 1) * 128] = mixed_ref[
-                pl.ds(i, local_rows, stride=lanes), :
+                pl.ds(lane_at(i), local_rows, stride=half_lanes), :
             ]
 
     more = spread(
         place,
-        lambda k: normed_send,
-        normed_send,
+        lambda k: normed_all.at[0, 0, 0],
         normed_all,
         row_sems,
+        lambda: None,
         lambda k: None,
-        widen,
-        widen,
+        lambda k: widen(k, 0),
+        lambda k: widen(k, 1),
         write_attention,
     )
     waits = waits + more
     for i in range(lanes):
         for r in range(local_rows):
             rows_ref[r * shards : (r + 1) * shards, i * 128 : (i + 1) * 128] = rows_wide[
-                pl.ds(r * lanes + i, shards, stride=size), :
+                pl.ds(lane_at(i) + r * half_lanes, shards, stride=size), :
             ].astype(jnp.bfloat16)
     half = down_ref.shape[0]
     projected_in = jnp.dot(rows_ref[...], gate_ref[...], preferred_element_type=f32)
-    split = picked(q_wide, local_rows, shards, 8)
-    weight = split[:, 0:1] + split[:, 64:65]
+    split = picked(own_wide, local_rows, shards, 16)
+    lane = lax.broadcasted_iota(jnp.int32, split.shape, 1)
+    weight = jnp.sum(jnp.where(lane % 64 == me // 2, split, 0.0), axis=1, keepdims=True)
     gate = projected_in[:, :half]
     activated = gate / (1.0 + jnp.exp(-gate)) * projected_in[:, half:]
     activated = jnp.where(weight != 0.0, activated * weight, 0.0).astype(jnp.bfloat16)
-    for i in range(0, width, 512):
-        scatter_rows(
-            jnp.dot(activated, down_ref[:, i : i + 512], preferred_element_type=f32), i // 128
-        )
-    expert_sum, more = collect(place, partial, size, second_boxes, second_sems, lambda: None)
+    total = Collect(place, partial, size, second_boxes, second_sems)
+    expert_sum, more = total.run(
+        lambda half: multiply_out(activated, down_ref, half), lambda: None
+    )
     waits = waits + more
     mixed_ref[...] = expert_sum
     for i in range(lanes):
-        expert_out[:, i * 128 : (i + 1) * 128] = mixed_ref[pl.ds(i, local_rows, stride=lanes), :]
-    for copy in waits + list(q_copies.values()):
-        copy.wait_send()
+        expert_out[:, i * 128 : (i + 1) * 128] = mixed_ref[pl.ds(lane_at(i), local_rows, stride=half_lanes), :]
+    for ref, sem in waits:
+        arrived(ref, sem)
 
 
 def fused_layer(
@@ -850,9 +885,17 @@
     column = shards // 8
     bf16, f32 = jnp.bfloat16, jnp.float32
     kv_rows = 2 * span + 16
+    half = size // 2
     boxes = [
-        pltpu.VMEM((count, size, 128), bf16)
-        for count in (shards // 2, shards // 2, shards // 2, shards // 2, column, column)
+        pltpu.VMEM(shape, bf16)
+        for shape in (
+            (2, column, 4, half, 128),
+            (2, column, 4, half, 128),
+            (2, column, 4, half, 128),
+            (2, column, 4, half, 128),
+            (2, column, half, 128),
+            (2, column, half, 128),
+        )
     ]
     operands = (
         prefix_of_row,
@@ -886,26 +929,25 @@
         ]
         + [
             pltpu.SemaphoreType.DMA((len(operands),)),
-            pltpu.VMEM((shards * 8, 128), f32),
-            pltpu.VMEM((shards, 8, 128), bf16),
-            pltpu.VMEM((column, 8, 8, 128), bf16),
-            pltpu.VMEM((column * 4, 2, 8, 128), bf16),
-            pltpu.VMEM((shards, 8, 128), bf16),
+            pltpu.VMEM((16, 128), f32),
+            pltpu.VMEM((shards, local_rows, 128), bf16),
+            pltpu.VMEM((column, 8, local_rows, 128), bf16),
+            pltpu.VMEM((column, 4, 2, local_rows, 128), bf16),
+            pltpu.VMEM((column, 4, local_rows, 128), bf16),
             pltpu.VMEM((shards * 8, 128), f32),
             pltpu.VMEM((own_key.shape[1] // HD, kv_rows, 128), bf16),
-            pltpu.VMEM((shards, kv_rows, 128), bf16),
+            pltpu.VMEM((column, 4, 2, kv_rows, 128), bf16),
             pltpu.VMEM((shards * 16, 128), f32),
             pltpu.VMEM((shards * local_rows, 128), f32),
             pltpu.VMEM((shards * size, 128), f32),
             pltpu.VMEM((size, 128), f32),
-            pltpu.VMEM((size, 128), bf16),
-            pltpu.VMEM((shards, size, 128), bf16),
+            pltpu.VMEM((column, 4, 2, size, 128), bf16),
             pltpu.VMEM((shards * size, 128), f32),
             pltpu.VMEM((shards * local_rows, width), bf16),
         ]
         + boxes
         + boxes
-        + [pltpu.SemaphoreType.DMA((shards,))] * 10,
+        + [pltpu.SemaphoreType.DMA((count,)) for count in (3, 4 * column + 2) * 5],
         compiler_params=pltpu.CompilerParams(
             collective_id=1, has_side_effects=True, vmem_limit_bytes=VMEM_BYTES
         ),
@@ -923,7 +965,9 @@
         and w_out.shape[0] == HD
         and width == shards * HD
         and w_out.shape[1] == width
-        and 2 * local_rows == 8
+        and local_rows == 4
+        and width % (256 * 16) == 0
+        and shards // 2 <= 64
         and shards % (own_key.shape[1] // HD * 8) == 0
         and shards * local_rows % CAND == 0
         and cache_keys.shape[1] % 16 == 0

time: 61.5 us -> 57.3 us (0.932)
  Pallas kernels: 59.1 us -> 55 us
    pallas_call x1, Pallas kernels: 59.1 us -> 55 us  [fused_layer(): pl.pallas_call(lambda *refs: layer_kernel(shards, CAND // local_rows, *re...]
where the time goes in v3:
time: 57.3 us; the launch traced here: 57.2 us
  Pallas kernels  55 us (96%)
  other arithmetic  1.57 us (3%)
  between operations  0.64 us (1%)
    pallas_call x1, Pallas kernels, fused_layer(): pl.pallas_call(lambda *refs: layer_kernel(shards, CAND // local_rows, *re...  55 us
    convert_element_type x1, other arithmetic, fused_layer(): return (mixed.astype(bf16), (mixed + expert_sum).astype(bf16))  1.57 us

profile of v3, /device:TPU:0, one launch (start us, length us, event | category | flops | bytes accessed | tf_op | source)
XLA Modules:
  0.0 57.2 jit_solution(2388425147332550942)
XLA Ops:
  0.6 55.0 %fused_layer.1 = (f32[4,4096]{1,0:T(4,128)}, f32[4,4096]{1,0:T(4,128)}) custom-call(s32[128]{0:T(128)} %refs_0_.1, s32[2]{0:T(128)} %refs_1_.1, bf16[2,32,256]{2,1,0:T(8,128)(2,1)} %refs_2_.1, bf16[2,32,256]{2,1,0:T(8,128)(2,1)} %refs_3_.1, bf16[4,256]{1,0:T(4,128)(2,1)} %refs_4_.1, bf16[4,256]{1,0:T(4,128)(2,1)} %refs_5_.1, bf16[4,4096]{1,0:T(4,128)(2,1)} %refs_6_.1, ...), custom_call_target="tpu_custom_call" | custom-call | tf_op jit(solution)/shard_map/fused_layer/pallas_call | solution.py:921
  55.6 1.6 %add_convert_fusion = (bf16[4,4096]{1,0:T(4,128)(2,1)}, bf16[4,4096]{1,0:T(4,128)(2,1)}) fusion(f32[4,4096]{1,0:T(4,128)} %get-tuple-element.4, f32[4,4096]{1,0:T(4,128)} %get-tuple-element.5), kind=kLoop, calls=%fused_computation | loop fusion | flops 49152 | bytes 196608 | tf_op jit(solution)/shard_map/convert_element_type | solution.py:956

commit v4 on v3

--- a/solution.py
+++ b/solution.py
@@ -440,8 +440,8 @@
 
     for k in reversed(range(1, column)):
         post(0, column_source(k), buffer.at[k, 0, 0], k, k * 8)
+        on_start(k)
     forward(0)
-    on_start()
     on_column(0)
     for k in range(1, column):
         arrived(buffer.at[k, 0, 0], recv_sem.at[k])
@@ -462,92 +462,171 @@
     ]
 
 
-class Collect:
-    def __init__(self, place, values, size, boxes, sems):
+def pieces_of(lanes):
+    part = lanes // 4
+    return ((0, part, True), (part, 2 * part, False), (3 * part, part, False))
+
+
+class Piece:
+    def __init__(self, place, values, size, local_rows, piece, boxes, sems):
         self.place, self.values, self.size = place, values, size
-        self.half = size // 2
+        self.first, self.rows = piece[0] * local_rows, piece[1] * local_rows
         self.core_out, self.core_in, self.plane_out, self.plane_in = boxes[0:4]
         self.column_out, self.column_in = boxes[4:6]
         self.kind = self.core_out.dtype
         self.send_sem, self.recv_sem = sems
-
-    def post(self, kind, slot, out_box, in_box, at, towards):
+        self.others = pl.ds(1, place.column - 1)
+
+    def post(self, kind, slot, source, target, towards):
         remote(
-            out_box.at[at],
-            in_box.at[at],
+            source,
+            target,
             self.send_sem.at[kind],
             self.recv_sem.at[slot],
             self.place.peer(towards),
         )
 
-    def slot(self, kind, half, k):
-        return (kind * 2 + half) * self.place.column + k
-
-    def held(self, half, pattern):
-        start = self.place.peer(pattern) * self.size + half * self.half
-        return self.values[pl.ds(pl.multiple_of(start, self.half), self.half), :]
-
-    def core(self, half):
+    def held(self, pattern):
+        start = self.place.peer(pattern) * self.size + self.first
+        return self.values[pl.ds(pl.multiple_of(start, 8), self.rows), :]
+
+    def core(self):
         for k in reversed(range(self.place.column)):
             for plane in range(4):
-                self.core_out[half, k, plane] = self.held(half, k * 8 + plane * 2 + 1).astype(
-                    self.kind
-                )
-            self.post(0, self.slot(0, half, k), self.core_out, self.core_in, (half, k), 1)
-
-    def chip(self, half, k, plane):
-        return self.held(half, k * 8 + plane * 2) + self.core_in[half, k, plane].astype(jnp.float32)
-
-    def plane(self, half, k):
-        arrived(self.core_in.at[half, k], self.recv_sem.at[self.slot(0, half, k)])
+                self.core_out[k, plane] = self.held(k * 8 + plane * 2 + 1).astype(self.kind)
+            self.post(0, k, self.core_out.at[k], self.core_in.at[k], 1)
+
+    def met(self, k):
+        arrived(self.core_in.at[k], self.recv_sem.at[k])
+
+    def chip(self, k, plane):
+        return self.held(k * 8 + plane * 2) + self.core_in[k, plane].astype(jnp.float32)
+
+
+class PlaneFirst(Piece):
+    def plane(self, k):
+        self.met(k)
         for plane in (3, 1, 2):
-            at = (half, k, plane)
-            self.plane_out[at] = self.chip(half, k, plane).astype(self.kind)
+            self.plane_out[k, plane] = self.chip(k, plane).astype(self.kind)
             self.post(
-                1, self.slot(1, half, k), self.plane_out, self.plane_in, at, plane * 2
+                1,
+                self.place.column + k,
+                self.plane_out.at[k, plane],
+                self.plane_in.at[k, plane],
+                plane * 2,
             )
 
-    def own(self, half, k):
-        total = self.chip(half, k, 0)
-        arrived(
-            self.plane_in.at[half, k, pl.ds(1, 3)], self.recv_sem.at[self.slot(1, half, k)]
+    def own(self, k):
+        total = self.chip(k, 0)
+        arrived(self.plane_in.at[k, pl.ds(1, 3)], self.recv_sem.at[self.place.column + k])
+        for plane in (1, 2, 3):
+            total = total + self.plane_in[k, plane].astype(jnp.float32)
+        return total
+
+    def column(self, k):
+        self.column_out[k] = self.own(k).astype(self.kind)
+        self.post(
+            2, 2 * self.place.column, self.column_out.at[k], self.column_in.at[k], k * 8
         )
+
+    def total(self):
+        value = self.own(0)
+        arrived(self.column_in.at[self.others], self.recv_sem.at[2 * self.place.column])
+        for k in range(1, self.place.column):
+            value = value + self.column_in[k].astype(jnp.float32)
+        return value
+
+    def sent(self):
+        return [
+            (self.core_out, self.send_sem.at[0]),
+            (self.plane_out.at[:, pl.ds(1, 3)], self.send_sem.at[1]),
+            (self.column_out.at[self.others], self.send_sem.at[2]),
+        ]
+
+
+class ColumnFirst(Piece):
+    def columns(self):
+        for k in reversed(range(1, self.place.column)):
+            self.met(k)
+            for plane in range(4):
+                self.column_out[k, plane] = self.chip(k, plane).astype(self.kind)
+            self.post(
+                2, self.place.column + 1, self.column_out.at[k], self.column_in.at[k], k * 8
+            )
+
+    def line(self, plane):
+        value = self.chip(0, plane)
+        for k in range(1, self.place.column):
+            value = value + self.column_in[k, plane].astype(jnp.float32)
+        return value
+
+    def planes(self):
+        self.met(0)
+        arrived(self.column_in.at[self.others], self.recv_sem.at[self.place.column + 1])
+        for plane in (3, 1, 2):
+            self.plane_out[plane] = self.line(plane).astype(self.kind)
+            self.post(
+                1,
+                self.place.column,
+                self.plane_out.at[plane],
+                self.plane_in.at[plane],
+                plane * 2,
+            )
+
+    def total(self):
+        value = self.line(0)
+        arrived(self.plane_in.at[pl.ds(1, 3)], self.recv_sem.at[self.place.column])
         for plane in (1, 2, 3):
-            total = total + self.plane_in[half, k, plane].astype(jnp.float32)
-        return total
-
-    def column(self, half, k):
-        at = (half, k)
-        self.column_out[at] = self.own(half, k).astype(self.kind)
-        self.post(
-            2, 4 * self.place.column + half, self.column_out, self.column_in, at, k * 8
+            value = value + self.plane_in[plane].astype(jnp.float32)
+        return value
+
+    def sent(self):
+        return [
+            (self.core_out, self.send_sem.at[0]),
+            (self.plane_out.at[pl.ds(1, 3)], self.send_sem.at[1]),
+            (self.column_out.at[self.others], self.send_sem.at[2]),
+        ]
+
+
+def collect(place, values, size, local_rows, boxes, sems, fill, filler):
+    pieces = pieces_of(size // local_rows)
+    made = [
+        (ColumnFirst if piece[2] else PlaneFirst)(
+            place,
+            values,
+            size,
+            local_rows,
+            piece,
+            boxes[6 * i : 6 * i + 6],
+            sems[2 * i : 2 * i + 2],
         )
-
-    def run(self, fill, filler):
-        steps = [(half, k) for k in reversed(range(1, self.place.column)) for half in range(2)]
-        fill(0)
-        self.core(0)
-        fill(1)
-        self.plane(*steps[0])
-        self.core(1)
-        for step in steps[1:] + [(0, 0), (1, 0)]:
-            self.plane(*step)
-        filler()
-        for step in steps:
-            self.column(*step)
-        totals = [self.own(half, 0) for half in range(2)]
-        others = pl.ds(1, self.place.column - 1)
-        for half in range(2):
-            arrived(
-                self.column_in.at[half, others], self.recv_sem.at[4 * self.place.column + half]
-            )
-            for k in range(1, self.place.column):
-                totals[half] = totals[half] + self.column_in[half, k].astype(jnp.float32)
-        return jnp.concatenate(totals, axis=0), [
-            (self.core_out, self.send_sem.at[0]),
-            (self.plane_out.at[:, :, pl.ds(1, 3)], self.send_sem.at[1]),
-            (self.column_out.at[:, others], self.send_sem.at[2]),
-        ]
+        for i, piece in enumerate(pieces)
+    ]
+    across, wide, rest = made
+    far = list(reversed(range(1, place.column)))
+    fill(0)
+    across.core()
+    fill(1)
+    across.columns()
+    wide.core()
+    fill(2)
+    wide.plane(far[0])
+    rest.core()
+    for k in far[1:]:
+        wide.plane(k)
+    for k in far:
+        rest.plane(k)
+    wide.plane(0)
+    rest.plane(0)
+    filler()
+    wide.column(far[0])
+    across.planes()
+    for k in far[1:]:
+        wide.column(k)
+    for k in far:
+        rest.column(k)
+    total = jnp.concatenate([piece.total() for piece in made], axis=0)
+    return total, [copy for piece in made for copy in piece.sent()]
 
 
 def layer_kernel(
@@ -593,9 +672,10 @@
         rows_ref,
     ) = refs[17 : 17 + 15]
     boxes_and_sems = refs[17 + 15 :]
-    first_boxes, second_boxes = boxes_and_sems[0:6], boxes_and_sems[6:12]
-    sems = boxes_and_sems[12:]
-    q_sems, kv_sems, first_sems, row_sems, second_sems = [sems[2 * i : 2 * i + 2] for i in range(5)]
+    first_boxes, second_boxes = boxes_and_sems[0:18], boxes_and_sems[18:36]
+    sems = boxes_and_sems[36:]
+    q_sems, kv_sems, row_sems = [sems[2 * i : 2 * i + 2] for i in range(3)]
+    first_sems, second_sems = sems[6:12], sems[12:18]
     place = Place(shards)
     me = place.me
     local_rows, width = queries_ref.shape
@@ -608,11 +688,12 @@
     per_group = shards // key_groups
     score_scale = 1.0 / math.sqrt(HD)
     f32 = jnp.float32
-    half_lanes = lanes // 2
-
-    def lane_at(i):
-        return i // half_lanes * (size // 2) + i % half_lanes
-
+    pieces = pieces_of(lanes)
+
+    def rows_of(i):
+        for first, count, _ in pieces:
+            if first <= i < first + count:
+                return first * local_rows + i - first, count
 
     place.greet()
     loads = []
@@ -663,11 +744,9 @@
     def q_post(kind, source, target, slot, towards):
         remote(source, target, q_sems[0].at[kind], q_sems[1].at[slot], place.peer(towards))
 
-    def q_start():
-        for k in reversed(range(1, column)):
-            first = place.peer(k * 8) // 8 * 8
-            q_post(0, q_send.at[pl.ds(first, 8)], q_column.at[k], k, k * 8)
-        q_column[0] = q_send[pl.ds(me // 8 * 8, 8)]
+    def q_start(k):
+        first = place.peer(k * 8) // 8 * 8
+        q_post(0, q_send.at[pl.ds(first, 8)], q_column.at[k], k, k * 8)
 
     def q_on_column(k):
         if k:
@@ -678,7 +757,8 @@
                 pl.ds(first + (0 if k else me // 8 * 8), 2)
             ]
             q_post(1, source, q_plane.at[k, plane], column + k, plane * 2)
-        q_plane[k, 0] = q_column[k, pl.ds(me % 8 // 2 * 2, 2)]
+        mine = me // 2 * 2
+        q_plane[k, 0] = q_column[k, pl.ds(mine % 8, 2)] if k else q_send[pl.ds(mine, 2)]
 
     def q_on_plane(k):
         arrived(q_plane.at[k, pl.ds(1, 3)], q_sems[1].at[column + k])
@@ -775,40 +855,56 @@
                 r * per_block : (r + 1) * per_block, :
             ]
 
-    def multiply_out(rows, matrix_ref, half):
-        for first in range(half * width // 2, (half + 1) * width // 2, 512):
+    def multiply_out(rows, matrix_ref, piece):
+        first, count, _ = pieces[piece]
+        for at in range(first, first + count, 4):
             result = jnp.dot(
-                rows, matrix_ref[:, first : first + 512], preferred_element_type=f32
+                rows, matrix_ref[:, at * 128 : (at + 4) * 128], preferred_element_type=f32
             )
             for i in range(4):
+                start, apart = rows_of(at + i)
                 for r in range(local_rows):
-                    start = lane_at(first // 128 + i) + r * half_lanes
-                    partial[pl.ds(start, shards, stride=size), :] = result[
+                    partial[pl.ds(start + r * apart, shards, stride=size), :] = result[
                         r * shards : (r + 1) * shards, i * 128 : (i + 1) * 128
                     ]
 
     loads[9].wait()
     head_rows = attended[...].astype(jnp.bfloat16)
-    total = Collect(place, partial, size, first_boxes, first_sems)
-    projected, more = total.run(
-        lambda half: multiply_out(head_rows, w_out_ref, half), dequantize_down
+    projected, more = collect(
+        place,
+        partial,
+        size,
+        local_rows,
+        first_boxes,
+        first_sems,
+        lambda piece: multiply_out(head_rows, w_out_ref, piece),
+        dequantize_down,
     )
     waits = waits + more
 
     loads[14].wait()
     loads[15].wait()
     for i in range(lanes):
-        mixed_ref[pl.ds(lane_at(i), local_rows, stride=half_lanes), :] = hidden_ref[
+        mixed_ref[pl.ds(rows_of(i)[0], local_rows, stride=rows_of(i)[1]), :] = hidden_ref[
             :, i * 128 : (i + 1) * 128
         ].astype(f32)
     mixed = mixed_ref[...] + projected
     mixed_ref[...] = mixed
-    grouped = mixed.reshape(2, local_rows, half_lanes, 128)
-    squares = jnp.sum(grouped * grouped, axis=2, keepdims=True)
-    squares = jnp.sum(jnp.sum(squares, axis=0, keepdims=True), axis=3, keepdims=True)
-    gain = gain_ref[...].reshape(2, 1, half_lanes, 128)
-    normed = grouped * lax.rsqrt(squares / width + EPSILON) * gain
-    normed_all[0, 0, 0] = normed.reshape(size, 128).astype(jnp.bfloat16)
+    grouped = [
+        mixed[first * local_rows : (first + count) * local_rows].reshape(local_rows, count, 128)
+        for first, count, _ in pieces
+    ]
+    squares = sum(jnp.sum(part * part, axis=1, keepdims=True) for part in grouped)
+    squares = jnp.sum(squares, axis=2, keepdims=True)
+    scale = lax.rsqrt(squares / width + EPSILON)
+    normed = jnp.concatenate(
+        [
+            (part * scale * gain_ref[first : first + count, :][None]).reshape(-1, 128)
+            for part, (first, count, _) in zip(grouped, pieces)
+        ],
+        axis=0,
+    )
+    normed_all[0, 0, 0] = normed.astype(jnp.bfloat16)
 
     def widen(k, core):
         for plane in range(4):
@@ -819,7 +915,7 @@
     def write_attention():
         for i in range(lanes):
             mixed_out[:, i * 128 : (i + 1) * 128] = mixed_ref[
-                pl.ds(lane_at(i), local_rows, stride=half_lanes), :
+                pl.ds(rows_of(i)[0], local_rows, stride=rows_of(i)[1]), :
             ]
 
     more = spread(
@@ -827,7 +923,7 @@
         lambda k: normed_all.at[0, 0, 0],
         normed_all,
         row_sems,
-        lambda: None,
+        lambda k: None,
         lambda k: None,
         lambda k: widen(k, 0),
         lambda k: widen(k, 1),
@@ -835,9 +931,10 @@
     )
     waits = waits + more
     for i in range(lanes):
+        start, apart = rows_of(i)
         for r in range(local_rows):
             rows_ref[r * shards : (r + 1) * shards, i * 128 : (i + 1) * 128] = rows_wide[
-                pl.ds(lane_at(i) + r * half_lanes, shards, stride=size), :
+                pl.ds(start + r * apart, shards, stride=size), :
             ].astype(jnp.bfloat16)
     half = down_ref.shape[0]
     projected_in = jnp.dot(rows_ref[...], gate_ref[...], preferred_element_type=f32)
@@ -847,14 +944,20 @@
     gate = projected_in[:, :half]
     activated = gate / (1.0 + jnp.exp(-gate)) * projected_in[:, half:]
     activated = jnp.where(weight != 0.0, activated * weight, 0.0).astype(jnp.bfloat16)
-    total = Collect(place, partial, size, second_boxes, second_sems)
-    expert_sum, more = total.run(
-        lambda half: multiply_out(activated, down_ref, half), lambda: None
+    expert_sum, more = collect(
+        place,
+        partial,
+        size,
+        local_rows,
+        second_boxes,
+        second_sems,
+        lambda piece: multiply_out(activated, down_ref, piece),
+        lambda: None,
     )
     waits = waits + more
     mixed_ref[...] = expert_sum
     for i in range(lanes):
-        expert_out[:, i * 128 : (i + 1) * 128] = mixed_ref[pl.ds(lane_at(i), local_rows, stride=half_lanes), :]
+        expert_out[:, i * 128 : (i + 1) * 128] = mixed_ref[pl.ds(rows_of(i)[0], local_rows, stride=rows_of(i)[1]), :]
     for ref, sem in waits:
         arrived(ref, sem)
 
@@ -885,18 +988,12 @@
     column = shards // 8
     bf16, f32 = jnp.bfloat16, jnp.float32
     kv_rows = 2 * span + 16
-    half = size // 2
-    boxes = [
-        pltpu.VMEM(shape, bf16)
-        for shape in (
-            (2, column, 4, half, 128),
-            (2, column, 4, half, 128),
-            (2, column, 4, half, 128),
-            (2, column, 4, half, 128),
-            (2, column, half, 128),
-            (2, column, half, 128),
-        )
-    ]
+    boxes = []
+    for _, count, column_first in pieces_of(lanes):
+        rows = count * local_rows
+        chips, line, plane = (column, 4, rows, 128), (column, rows, 128), (4, rows, 128)
+        last = (plane, plane, chips, chips) if column_first else (chips, chips, line, line)
+        boxes = boxes + [pltpu.VMEM(shape, bf16) for shape in (chips, chips) + last]
     operands = (
         prefix_of_row,
         context_len,
@@ -947,7 +1044,11 @@
         ]
         + boxes
         + boxes
-        + [pltpu.SemaphoreType.DMA((count,)) for count in (3, 4 * column + 2) * 5],
+        + [
+            pltpu.SemaphoreType.DMA((count,))
+            for count in (3, 2 * column + 1, 3, 3 * column, 3, 3 * column)
+            + (3, column + 2, 3, 2 * column + 1, 3, 2 * column + 1) * 2
+        ],
         compiler_params=pltpu.CompilerParams(
             collective_id=1, has_side_effects=True, vmem_limit_bytes=VMEM_BYTES
         ),
@@ -966,7 +1067,7 @@
         and width == shards * HD
         and w_out.shape[1] == width
         and local_rows == 4
-        and width % (256 * 16) == 0
+        and width % (128 * 32) == 0
         and shards // 2 <= 64
         and shards % (own_key.shape[1] // HD * 8) == 0
         and shards * local_rows % CAND == 0

time: 57.3 us -> 56.5 us (0.986)
  Pallas kernels: 55 us -> 54.1 us
    pallas_call x1, Pallas kernels: 55 us -> 54.1 us  [fused_layer(): pl.pallas_call(lambda *refs: layer_kernel(shards, CAND // local_rows, *re...]
where the time goes in v4:
time: 56.5 us; the launch traced here: 56.3 us
  Pallas kernels  54.1 us (96%)
  other arithmetic  1.57 us (3%)
  between operations  0.64 us (1%)
    pallas_call x1, Pallas kernels, fused_layer(): pl.pallas_call(lambda *refs: layer_kernel(shards, CAND // local_rows, *re...  54.1 us
    convert_element_type x1, other arithmetic, fused_layer(): return (mixed.astype(bf16), (mixed + expert_sum).astype(bf16))  1.57 us

profile of v4, /device:TPU:0, one launch (start us, length us, event | category | flops | bytes accessed | tf_op | source)
XLA Modules:
  0.0 56.3 jit_solution(16156559355646233747)
XLA Ops:
  0.6 54.1 %fused_layer.1 = (f32[4,4096]{1,0:T(4,128)}, f32[4,4096]{1,0:T(4,128)}) custom-call(s32[128]{0:T(128)} %refs_0_.1, s32[2]{0:T(128)} %refs_1_.1, bf16[2,32,256]{2,1,0:T(8,128)(2,1)} %refs_2_.1, bf16[2,32,256]{2,1,0:T(8,128)(2,1)} %refs_3_.1, bf16[4,256]{1,0:T(4,128)(2,1)} %refs_4_.1, bf16[4,256]{1,0:T(4,128)(2,1)} %refs_5_.1, bf16[4,4096]{1,0:T(4,128)(2,1)} %refs_6_.1, ...), custom_call_target="tpu_custom_call" | custom-call | tf_op jit(solution)/shard_map/fused_layer/pallas_call | solution.py:1018
  54.8 1.6 %add_convert_fusion = (bf16[4,4096]{1,0:T(4,128)(2,1)}, bf16[4,4096]{1,0:T(4,128)(2,1)}) fusion(f32[4,4096]{1,0:T(4,128)} %get-tuple-element.4, f32[4,4096]{1,0:T(4,128)} %get-tuple-element.5), kind=kLoop, calls=%fused_computation | loop fusion | flops 49152 | bytes 196608 | tf_op jit(solution)/shard_map/convert_element_type | solution.py:1057

commit v5 on v4

--- a/solution.py
+++ b/solution.py
@@ -14,6 +14,8 @@
 NEG = -1e30
 EPSILON = 1e-06
 VMEM_BYTES = None
+ACROSS = 2
+REST = 3
 
 
 def swapped(value, axis, distance):
@@ -463,8 +465,10 @@
 
 
 def pieces_of(lanes):
-    part = lanes // 4
-    return ((0, part, True), (part, 2 * part, False), (3 * part, part, False))
+    part = lanes // 8
+    across, rest = ACROSS * part, REST * part
+    wide = lanes - across - rest
+    return ((0, across, True), (across, wide, False), (across + wide, rest, False))
 
 
 class Piece:
@@ -606,25 +610,27 @@
     far = list(reversed(range(1, place.column)))
     fill(0)
     across.core()
+    fill(2)
+    rest.core()
+    across.columns()
     fill(1)
-    across.columns()
+    for k in far[:2]:
+        rest.plane(k)
     wide.core()
-    fill(2)
-    wide.plane(far[0])
-    rest.core()
-    for k in far[1:]:
+    for k in far[2:]:
+        rest.plane(k)
+    for k in far:
         wide.plane(k)
+    rest.plane(0)
+    wide.plane(0)
+    filler()
+    rest.column(far[0])
+    rest.column(far[1])
+    across.planes()
+    for k in far[2:]:
+        rest.column(k)
     for k in far:
-        rest.plane(k)
-    wide.plane(0)
-    rest.plane(0)
-    filler()
-    wide.column(far[0])
-    across.planes()
-    for k in far[1:]:
         wide.column(k)
-    for k in far:
-        rest.column(k)
     total = jnp.concatenate([piece.total() for piece in made], axis=0)
     return total, [copy for piece in made for copy in piece.sent()]
 
@@ -667,11 +673,12 @@
         attended,
         partial,
         mixed_ref,
+        normed_ref,
         normed_all,
         rows_wide,
         rows_ref,
-    ) = refs[17 : 17 + 15]
-    boxes_and_sems = refs[17 + 15 :]
+    ) = refs[17 : 17 + 16]
+    boxes_and_sems = refs[17 + 16 :]
     first_boxes, second_boxes = boxes_and_sems[0:18], boxes_and_sems[18:36]
     sems = boxes_and_sems[36:]
     q_sems, kv_sems, row_sems = [sems[2 * i : 2 * i + 2] for i in range(3)]
@@ -689,11 +696,6 @@
     score_scale = 1.0 / math.sqrt(HD)
     f32 = jnp.float32
     pieces = pieces_of(lanes)
-
-    def rows_of(i):
-        for first, count, _ in pieces:
-            if first <= i < first + count:
-                return first * local_rows + i - first, count
 
     place.greet()
     loads = []
@@ -862,9 +864,8 @@
                 rows, matrix_ref[:, at * 128 : (at + 4) * 128], preferred_element_type=f32
             )
             for i in range(4):
-                start, apart = rows_of(at + i)
                 for r in range(local_rows):
-                    partial[pl.ds(start + r * apart, shards, stride=size), :] = result[
+                    partial[pl.ds((at + i) * local_rows + r, shards, stride=size), :] = result[
                         r * shards : (r + 1) * shards, i * 128 : (i + 1) * 128
                     ]
 
@@ -885,26 +886,18 @@
     loads[14].wait()
     loads[15].wait()
     for i in range(lanes):
-        mixed_ref[pl.ds(rows_of(i)[0], local_rows, stride=rows_of(i)[1]), :] = hidden_ref[
+        mixed_ref[i * local_rows : (i + 1) * local_rows, :] = hidden_ref[
             :, i * 128 : (i + 1) * 128
         ].astype(f32)
     mixed = mixed_ref[...] + projected
     mixed_ref[...] = mixed
-    grouped = [
-        mixed[first * local_rows : (first + count) * local_rows].reshape(local_rows, count, 128)
-        for first, count, _ in pieces
-    ]
-    squares = sum(jnp.sum(part * part, axis=1, keepdims=True) for part in grouped)
-    squares = jnp.sum(squares, axis=2, keepdims=True)
-    scale = lax.rsqrt(squares / width + EPSILON)
-    normed = jnp.concatenate(
-        [
-            (part * scale * gain_ref[first : first + count, :][None]).reshape(-1, 128)
-            for part, (first, count, _) in zip(grouped, pieces)
-        ],
-        axis=0,
-    )
-    normed_all[0, 0, 0] = normed.astype(jnp.bfloat16)
+    for r in range(local_rows):
+        row = mixed_ref[pl.ds(r, lanes, stride=local_rows), :]
+        squares = jnp.sum(jnp.sum(row * row, axis=0, keepdims=True), axis=1, keepdims=True)
+        normed_ref[pl.ds(r, lanes, stride=local_rows), :] = (
+            row * lax.rsqrt(squares / width + EPSILON) * gain_ref[...]
+        )
+    normed_all[0, 0, 0] = normed_ref[...].astype(jnp.bfloat16)
 
     def widen(k, core):
         for plane in range(4):
@@ -915,7 +908,7 @@
     def write_attention():
         for i in range(lanes):
             mixed_out[:, i * 128 : (i + 1) * 128] = mixed_ref[
-                pl.ds(rows_of(i)[0], local_rows, stride=rows_of(i)[1]), :
+                i * local_rows : (i + 1) * local_rows, :
             ]
 
     more = spread(
@@ -931,10 +924,9 @@
     )
     waits = waits + more
     for i in range(lanes):
-        start, apart = rows_of(i)
         for r in range(local_rows):
             rows_ref[r * shards : (r + 1) * shards, i * 128 : (i + 1) * 128] = rows_wide[
-                pl.ds(start + r * apart, shards, stride=size), :
+                pl.ds(i * local_rows + r, shards, stride=size), :
             ].astype(jnp.bfloat16)
     half = down_ref.shape[0]
     projected_in = jnp.dot(rows_ref[...], gate_ref[...], preferred_element_type=f32)
@@ -957,7 +949,7 @@
     waits = waits + more
     mixed_ref[...] = expert_sum
     for i in range(lanes):
-        expert_out[:, i * 128 : (i + 1) * 128] = mixed_ref[pl.ds(rows_of(i)[0], local_rows, stride=rows_of(i)[1]), :]
+        expert_out[:, i * 128 : (i + 1) * 128] = mixed_ref[i * local_rows : (i + 1) * local_rows, :]
     for ref, sem in waits:
         arrived(ref, sem)
 
@@ -1038,6 +1030,7 @@
             pltpu.VMEM((shards * local_rows, 128), f32),
             pltpu.VMEM((shards * size, 128), f32),
             pltpu.VMEM((size, 128), f32),
+            pltpu.VMEM((size, 128), f32),
             pltpu.VMEM((column, 4, 2, size, 128), bf16),
             pltpu.VMEM((shards * size, 128), f32),
             pltpu.VMEM((shards * local_rows, width), bf16),

time: 56.5 us -> 55.1 us (0.975)
  Pallas kernels: 54.1 us -> 52.7 us
    pallas_call x1, Pallas kernels: 54.1 us -> 52.7 us  [fused_layer(): pl.pallas_call(lambda *refs: layer_kernel(shards, CAND // local_rows, *re...]
where the time goes in v5:
time: 55.1 us; the launch traced here: 54.9 us
  Pallas kernels  52.7 us (96%)
  other arithmetic  1.57 us (3%)
  between operations  0.64 us (1%)
    pallas_call x1, Pallas kernels, fused_layer(): pl.pallas_call(lambda *refs: layer_kernel(shards, CAND // local_rows, *re...  52.7 us
    convert_element_type x1, other arithmetic, fused_layer(): return (mixed.astype(bf16), (mixed + expert_sum).astype(bf16))  1.57 us

profile of v5, /device:TPU:0, one launch (start us, length us, event | category | flops | bytes accessed | tf_op | source)
XLA Modules:
  0.0 54.9 jit_solution(1427785797197907340)
XLA Ops:
  0.6 52.7 %fused_layer.1 = (f32[4,4096]{1,0:T(4,128)}, f32[4,4096]{1,0:T(4,128)}) custom-call(s32[128]{0:T(128)} %refs_0_.1, s32[2]{0:T(128)} %refs_1_.1, bf16[2,32,256]{2,1,0:T(8,128)(2,1)} %refs_2_.1, bf16[2,32,256]{2,1,0:T(8,128)(2,1)} %refs_3_.1, bf16[4,256]{1,0:T(4,128)(2,1)} %refs_4_.1, bf16[4,256]{1,0:T(4,128)(2,1)} %refs_5_.1, bf16[4,4096]{1,0:T(4,128)(2,1)} %refs_6_.1, ...), custom_call_target="tpu_custom_call" | custom-call | tf_op jit(solution)/shard_map/fused_layer/pallas_call | solution.py:1010
  53.3 1.6 %add_convert_fusion = (bf16[4,4096]{1,0:T(4,128)(2,1)}, bf16[4,4096]{1,0:T(4,128)(2,1)}) fusion(f32[4,4096]{1,0:T(4,128)} %get-tuple-element.4, f32[4,4096]{1,0:T(4,128)} %get-tuple-element.5), kind=kLoop, calls=%fused_computation | loop fusion | flops 49152 | bytes 196608 | tf_op jit(solution)/shard_map/convert_element_type | solution.py:1050

commit v6 on v5

--- a/solution.py
+++ b/solution.py
@@ -441,14 +441,14 @@
             post(1, buffer.at[k, 0, 0], buffer.at[k, plane, 0], column + k, plane * 2)
 
     for k in reversed(range(1, column)):
+        on_start(k)
         post(0, column_source(k), buffer.at[k, 0, 0], k, k * 8)
-        on_start(k)
+    on_column(0)
     forward(0)
-    on_column(0)
     for k in range(1, column):
+        on_column(k)
         arrived(buffer.at[k, 0, 0], recv_sem.at[k])
         forward(k)
-        on_column(k)
     filler()
     for k in range(column):
         arrived(buffer.at[k, pl.ds(1, 3), 0], recv_sem.at[column + k])

time: 55.1 us -> 55.2 us (level)
  no operation moved by 1% of the time
where the time goes in v6:
time: 55.2 us; the launch traced here: 55 us
  Pallas kernels  52.8 us (96%)
  other arithmetic  1.57 us (3%)
  between operations  0.64 us (1%)
    pallas_call x1, Pallas kernels, fused_layer(): pl.pallas_call(lambda *refs: layer_kernel(shards, CAND // local_rows, *re...  52.8 us
    convert_element_type x1, other arithmetic, fused_layer(): return (mixed.astype(bf16), (mixed + expert_sum).astype(bf16))  1.57 us

profile of v6, /device:TPU:0, one launch (start us, length us, event | category | flops | bytes accessed | tf_op | source)
XLA Modules:
  0.0 55.0 jit_solution(8553384556559952543)
XLA Ops:
  0.6 52.8 %fused_layer.1 = (f32[4,4096]{1,0:T(4,128)}, f32[4,4096]{1,0:T(4,128)}) custom-call(s32[128]{0:T(128)} %refs_0_.1, s32[2]{0:T(128)} %refs_1_.1, bf16[2,32,256]{2,1,0:T(8,128)(2,1)} %refs_2_.1, bf16[2,32,256]{2,1,0:T(8,128)(2,1)} %refs_3_.1, bf16[4,256]{1,0:T(4,128)(2,1)} %refs_4_.1, bf16[4,256]{1,0:T(4,128)(2,1)} %refs_5_.1, bf16[4,4096]{1,0:T(4,128)(2,1)} %refs_6_.1, ...), custom_call_target="tpu_custom_call" | custom-call | tf_op jit(solution)/shard_map/fused_layer/pallas_call | solution.py:1010
  53.5 1.6 %add_convert_fusion = (bf16[4,4096]{1,0:T(4,128)(2,1)}, bf16[4,4096]{1,0:T(4,128)(2,1)}) fusion(f32[4,4096]{1,0:T(4,128)} %get-tuple-element.4, f32[4,4096]{1,0:T(4,128)} %get-tuple-element.5), kind=kLoop, calls=%fused_computation | loop fusion | flops 49152 | bytes 196608 | tf_op jit(solution)/shard_map/convert_element_type | solution.py:1050
